TPU v7x, 32 devices: a whole 2x2x4 slice. The times are simulated.
32 devices in a mesh: ctx: 8 (over z, x), exp: 4 (over y, core).
Axes of the slice: x: 2, y: 2, z: 4, core: 2. Of those that a mesh axis runs over, the one named last changes fastest.
Arguments:
- tokens: bfloat16 [2, 4, 1024, 1024], P(None, 'exp', 'ctx'), may hold values from -6 to 6
- cotangent: bfloat16 [2, 4, 1024, 1024], P(None, 'exp', 'ctx'), may hold values from -6 to 6
- bucket_ids: int32 [2048], replicated, may hold values from 0 to 31
- routes: int32 [2, 4, 1024, 2], P(None, 'exp', 'ctx'), may hold values from 0 to 3, all different within a row; in each aligned block of 128 rows (0 to 127, 128 to 255, ..., all dimensions but the last counted through in order) at most 80 rows name the same one
- qkv_master: float32 [3, 1024, 1024], P(None, ('ctx', 'exp')), may hold values from -0.1875 to 0.1875
- out_master: float32 [1024, 1024], P(('ctx', 'exp')), may hold values from -1.5 to 1.5
- router_master: float32 [1024, 4], P(('ctx', 'exp')), may hold values from -0.375 to 0.375
- gain_attn_master: float32 [1024], P(('ctx', 'exp')), may hold values from 0.5 to 1.5
- gain_mix_master: float32 [1024], P(('ctx', 'exp')), may hold values from 0.5 to 1.5
- table_master: float32 [512], P(('ctx', 'exp')), may hold values from -4 to 4
- gate_master: float32 [4, 1024, 2816], P('exp', 'ctx'), may hold values from -0.1875 to 0.1875
- up_master: float32 [4, 1024, 2816], P('exp', 'ctx'), may hold values from -0.1875 to 0.1875
- down_master: float32 [4, 2816, 1024], P('exp', 'ctx'), may hold values from -0.109375 to 0.109375
- qkv_first: float32 [3, 1024, 1024], P(None, ('ctx', 'exp')), may hold values from -543.058 to 543.058
- out_first: float32 [1024, 1024], P(('ctx', 'exp')), may hold values from -13.57645 to 13.57645
- router_first: float32 [1024, 4], P(('ctx', 'exp')), may hold values from -814.58701 to 814.58701
- gain_attn_first: float32 [1024], P(('ctx', 'exp')), may hold values from -2715.29 to 2715.29
- gain_mix_first: float32 [1024], P(('ctx', 'exp')), may hold values from -271.529 to 271.529
- table_first: float32 [512], P(('ctx', 'exp')), may hold values from -814.58701 to 814.58701
- gate_first: float32 [4, 1024, 2816], P('exp', 'ctx'), may hold values from -27.1529 to 27.1529
- up_first: float32 [4, 1024, 2816], P('exp', 'ctx'), may hold values from -27.1529 to 27.1529
- down_first: float32 [4, 2816, 1024], P('exp', 'ctx'), may hold values from -54.3058 to 54.3058
- qkv_second: float32 [3, 1024, 1024], P(None, ('ctx', 'exp')), may hold values from 9830.4 to 98304
- out_second: float32 [1024, 1024], P(('ctx', 'exp')), may hold values from 6.144 to 61.44
- router_second: float32 [1024, 4], P(('ctx', 'exp')), may hold values from 22118.4 to 221184
- gain_attn_second: float32 [1024], P(('ctx', 'exp')), may hold values from 245760 to 2457600
- gain_mix_second: float32 [1024], P(('ctx', 'exp')), may hold values from 2457.6 to 24576
- table_second: float32 [512], P(('ctx', 'exp')), may hold values from 22118.4 to 221184
- gate_second: float32 [4, 1024, 2816], P('exp', 'ctx'), may hold values from 24.576 to 245.76
- up_second: float32 [4, 1024, 2816], P('exp', 'ctx'), may hold values from 24.576 to 245.76
- down_second: float32 [4, 2816, 1024], P('exp', 'ctx'), may hold values from 98.304 to 983.04
Outputs:
- output: bfloat16 [2, 4, 1024, 1024], P(None, 'exp', 'ctx')
- grad_tokens: float32 [2, 4, 1024, 1024], P(None, 'exp', 'ctx')
- qkv_grad: float32 [3, 1024, 1024], P(None, ('ctx', 'exp'))
- out_grad: float32 [1024, 1024], P(('ctx', 'exp'))
- router_grad: float32 [1024, 4], P(('ctx', 'exp'))
- gain_attn_grad: float32 [1024], P(('ctx', 'exp'))
- gain_mix_grad: float32 [1024], P(('ctx', 'exp'))
- table_grad: float32 [512], P(('ctx', 'exp'))
- gate_grad: float32 [4, 1024, 2816], P('exp', 'ctx')
- up_grad: float32 [4, 1024, 2816], P('exp', 'ctx')
- down_grad: float32 [4, 2816, 1024], P('exp', 'ctx')
- qkv_first_new: float32 [3, 1024, 1024], P(None, ('ctx', 'exp'))
- out_first_new: float32 [1024, 1024], P(('ctx', 'exp'))
- router_first_new: float32 [1024, 4], P(('ctx', 'exp'))
- gain_attn_first_new: float32 [1024], P(('ctx', 'exp'))
- gain_mix_first_new: float32 [1024], P(('ctx', 'exp'))
- table_first_new: float32 [512], P(('ctx', 'exp'))
- gate_first_new: float32 [4, 1024, 2816], P('exp', 'ctx')
- up_first_new: float32 [4, 1024, 2816], P('exp', 'ctx')
- down_first_new: float32 [4, 2816, 1024], P('exp', 'ctx')
- qkv_second_new: float32 [3, 1024, 1024], P(None, ('ctx', 'exp'))
- out_second_new: float32 [1024, 1024], P(('ctx', 'exp'))
- router_second_new: float32 [1024, 4], P(('ctx', 'exp'))
- gain_attn_second_new: float32 [1024], P(('ctx', 'exp'))
- gain_mix_second_new: float32 [1024], P(('ctx', 'exp'))
- table_second_new: float32 [512], P(('ctx', 'exp'))
- gate_second_new: float32 [4, 1024, 2816], P('exp', 'ctx')
- up_second_new: float32 [4, 1024, 2816], P('exp', 'ctx')
- down_second_new: float32 [4, 2816, 1024], P('exp', 'ctx')
- qkv_update: float32 [3, 1024, 1024], P(None, ('ctx', 'exp'))
- out_update: float32 [1024, 1024], P(('ctx', 'exp'))
- router_update: float32 [1024, 4], P(('ctx', 'exp'))
- gain_attn_update: float32 [1024], P(('ctx', 'exp'))
- gain_mix_update: float32 [1024], P(('ctx', 'exp'))
- table_update: float32 [512], P(('ctx', 'exp'))
- gate_update: float32 [4, 1024, 2816], P('exp', 'ctx')
- up_update: float32 [4, 1024, 2816], P('exp', 'ctx')
- down_update: float32 [4, 2816, 1024], P('exp', 'ctx')
Inputs may be any that keep to these rules, and one draw needn't show every extreme that they name: `routes`: in each aligned block of 128 tokens (one index of ctx, one sequence) no expert is named by more than 80 choices, and in some block one expert is named exactly 80 times; the two experts of a token differ.
All inputs are finite; a program needn't handle non-finite values.
Results may differ from a plain program's by a relative error of at most 0.024.
The roundings to bfloat16 on the way count: a program that leaves them out, or rounds other values in their place, can miss the bound.
Values may be sent and summed in bfloat16 or wider, within the bound.
A program may use at most 256 MiB of HBM per device.

v0:
```python
from functools import partial
import math

import jax
import jax.numpy as jnp
from jax import lax
from jax.experimental import pallas as pl
from jax.experimental.pallas import tpu as pltpu
from jax.sharding import PartitionSpec as P

D = 1024
HEADS = 16
HEAD_DIM = 64
TOP = 2
BLOCK = 256
STEP = 3
EXP_AXIS = 4

eps_norm = 1e-06
eps_adam = 1e-08
score_scale = 0.125
decay_rate = 0.5
learn_rate = 1.0
weight_decay = 0.1
highest = lax.Precision.HIGHEST
last_dims = (((1,), (1,)), ((), ()))
first_dims = (((0,), (0,)), ((), ()))
bf16 = jnp.bfloat16
f32 = jnp.float32
both = ("ctx", "exp")
MESH = pl.DeviceIdType.MESH


def swap_bit(value, bit):
    count = lax.axis_size("ctx") * EXP_AXIS
    return lax.ppermute(value, both, [(d, d ^ (1 << bit)) for d in range(count)])


def flat_index():
    return lax.axis_index("ctx") * EXP_AXIS + lax.axis_index("exp")


def my_bit(bit):
    return (flat_index() >> bit) & 1


def turn(value):
    count = lax.axis_size("ctx") * EXP_AXIS

    def other(d):
        low, high = d & 1, (d >> 2) & 1
        return (d & ~5) | (low << 2) | high

    got = lax.ppermute(value, both, [(d, other(d)) for d in range(count) if other(d) != d])
    return jnp.where(my_bit(0) == my_bit(2), value, got)


def place_of(flat):
    return (flat // EXP_AXIS, flat % EXP_AXIS)


def greet(partners):
    barrier = pltpu.get_barrier_semaphore()
    for partner in partners:
        pl.semaphore_signal(barrier, inc=1, device_id=place_of(partner), device_id_type=MESH)
    pl.semaphore_wait(barrier, len(partners))


def remote(source, target, send, recv, partner):
    return pltpu.make_async_remote_copy(
        src_ref=source, dst_ref=target, send_sem=send, recv_sem=recv,
        device_id=place_of(partner), device_id_type=MESH,
    )


def exchange_call(kernel, number, arrays, shapes, sems):
    vmem = pl.BlockSpec(memory_space=pltpu.VMEM)
    sent = sum(array.size * array.dtype.itemsize for array in arrays)
    return pl.pallas_call(
        kernel,
        in_specs=[vmem] * len(arrays),
        out_specs=[vmem] * len(shapes),
        out_shape=shapes,
        scratch_shapes=[pltpu.SemaphoreType.DMA((size,)) for size in sems],
        compiler_params=pltpu.CompilerParams(
            collective_id=number, has_side_effects=True, vmem_limit_bytes=48 << 20
        ),
        cost_estimate=pl.CostEstimate(flops=0, bytes_accessed=8 * sent, transcendentals=0),
    )(*arrays)


def opening_kernel(cycle, group, tok_ref, col_ref, seq_ref, all_ref, s1, r1, s2, r2, s3, r3, s4, r4):
    me = flat_index()
    ctx, exp = place_of(me)
    greet([me ^ (rel * EXP_AXIS) for rel in range(1, cycle)] + [me ^ rel for rel in range(1, EXP_AXIS)])
    mine = ctx // group
    copies, relays, tokens, forwards = [], [], [], []
    for rel in range(1, cycle):
        peer = ctx ^ rel
        copies.append(
            remote(
                col_ref.at[lax.rem(peer, group)], all_ref.at[exp, ctx], s1.at[rel], r1.at[rel],
                me ^ (rel * EXP_AXIS),
            )
        )
    for far in range(group, cycle, group):
        relays.append(
            remote(
                tok_ref.at[mine ^ (far // group)], seq_ref.at[ctx], s2.at[far // group],
                r2.at[far // group], me ^ (far * EXP_AXIS),
            )
        )
    for rel in range(1, group):
        tokens.append(
            remote(
                tok_ref.at[mine], seq_ref.at[ctx], s3.at[rel], r3.at[rel], me ^ (rel * EXP_AXIS)
            )
        )
    for copy in copies + relays + tokens:
        copy.start()
    all_ref[exp, ctx] = col_ref[lax.rem(ctx, group)]
    seq_ref[ctx] = tok_ref[mine]
    for far, copy in zip(range(group, cycle, group), relays):
        copy.wait_recv()
        for rel in range(1, group):
            slot = far + rel
            tokens.append(
                remote(
                    seq_ref.at[ctx ^ far], seq_ref.at[ctx ^ far], s3.at[slot], r3.at[slot],
                    me ^ (rel * EXP_AXIS),
                )
            )
            tokens[-1].start()
    for copy in copies:
        copy.wait()
    for rel in range(1, EXP_AXIS):
        forwards.append(
            remote(all_ref.at[exp], all_ref.at[exp], s4.at[rel], r4.at[rel], me ^ rel)
        )
        forwards[-1].start()
    for copy in relays:
        copy.wait_send()
    for copy in tokens + forwards:
        copy.wait()


def opening(tok, cols):
    cycle = lax.axis_size("ctx")
    group = cycle // tok.shape[0]
    return exchange_call(
        partial(opening_kernel, cycle, group), 0, [tok, cols],
        [
            jax.ShapeDtypeStruct((cycle,) + tok.shape[1:], tok.dtype),
            jax.ShapeDtypeStruct((EXP_AXIS, cycle) + cols.shape[1:], cols.dtype),
        ],
        [cycle, cycle, cycle, cycle, cycle, cycle, EXP_AXIS, EXP_AXIS],
    )


def cycle_kernel(cycle, in_ref, out_ref, send, recv):
    me = flat_index()
    ctx, _ = place_of(me)
    greet([me ^ (rel * EXP_AXIS) for rel in range(1, cycle)])
    copies = []
    for rel in range(1, cycle):
        copies.append(
            remote(
                in_ref.at[ctx ^ rel], out_ref.at[ctx], send.at[rel], recv.at[rel],
                me ^ (rel * EXP_AXIS),
            )
        )
        copies[-1].start()
    out_ref[ctx] = in_ref[ctx]
    for copy in copies:
        copy.wait()


def cycle_swap(value, number):
    cycle = lax.axis_size("ctx")
    return exchange_call(
        partial(cycle_kernel, cycle), number, [value],
        [jax.ShapeDtypeStruct(value.shape, value.dtype)], [cycle, cycle],
    )[0]


def closing_kernel(cycle, col_ref, out_in, small_ref, col_out, out_out, all_ref, s1, r1, s2, r2, s3, r3):
    me = flat_index()
    ctx, _ = place_of(me)
    count = cycle * EXP_AXIS
    greet([me ^ rel for rel in range(1, count)])
    copies = []
    for source, target, send, recv in ((col_ref, col_out, s1, r1), (out_in, out_out, s2, r2)):
        for rel in range(1, cycle):
            copies.append(
                remote(
                    source.at[ctx ^ rel], target.at[ctx], send.at[rel], recv.at[rel],
                    me ^ (rel * EXP_AXIS),
                )
            )
    for rel in range(1, count):
        copies.append(
            remote(small_ref.at[me ^ rel], all_ref.at[me], s3.at[rel], r3.at[rel], me ^ rel)
        )
    for copy in copies:
        copy.start()
    col_out[ctx] = col_ref[ctx]
    out_out[ctx] = out_in[ctx]
    all_ref[me] = small_ref[me]
    for copy in copies:
        copy.wait()


def closing(cols, out, small):
    cycle = lax.axis_size("ctx")
    count = cycle * EXP_AXIS
    return exchange_call(
        partial(closing_kernel, cycle), 6, [cols, out, small],
        [jax.ShapeDtypeStruct(x.shape, x.dtype) for x in (cols, out, small)],
        [cycle, cycle, cycle, cycle, count, count],
    )


def plane_kernel(forward, arrays, *refs):
    ins, outs, send, recv = refs[:arrays], refs[arrays : 2 * arrays], refs[-2], refs[-1]
    me = flat_index()
    ctx, exp = place_of(me)
    greet([me ^ rel for rel in range(1, 2 * EXP_AXIS)])
    base = (ctx // 2) * 2
    ctx_low, exp_low = lax.rem(ctx, 2), lax.rem(exp, 2)
    for index in range(arrays):
        for e in range(EXP_AXIS):
            own = jnp.logical_and(exp == e, ctx_low == exp_low)
            sem = index * EXP_AXIS
            if forward:
                to_ctx, to_exp = base + e % 2, (e // 2) * 2 + ctx_low
                slot = exp
            else:
                to_ctx, to_exp = base + exp_low, e
                slot = (exp // 2) * 2 + ctx_low
            copy = remote(
                ins[index].at[e], outs[index].at[slot], send.at[sem + e], recv.at[sem + slot],
                to_ctx * EXP_AXIS + to_exp,
            )

            @pl.when(jnp.logical_not(own))
            def _():
                copy.start()

            @pl.when(own)
            def _():
                outs[index][e] = ins[index][e]

    for index in range(arrays):
        for e in range(EXP_AXIS):
            own = jnp.logical_and(exp == e, ctx_low == exp_low)
            sem = index * EXP_AXIS + e
            done = remote(ins[index].at[e], outs[index].at[e], send.at[sem], recv.at[sem], me ^ 1)

            @pl.when(jnp.logical_not(own))
            def _():
                done.wait()


def plane_swap(values, forward, number):
    count = len(values)
    return exchange_call(
        partial(plane_kernel, forward, count), number, list(values),
        [jax.ShapeDtypeStruct(x.shape, x.dtype) for x in values],
        [count * EXP_AXIS, count * EXP_AXIS],
    )


def line_permute(value, step, start):
    size = lax.axis_size("ctx") // 2
    pairs = []
    for a in range(size):
        b = a + step
        if 0 <= b < size and (a >= start if step > 0 else a < size - start):
            for low in range(2 * EXP_AXIS):
                pairs.append((a * 2 * EXP_AXIS + low, b * 2 * EXP_AXIS + low))
    return lax.ppermute(value, both, pairs)


def cube_sum(value, bit):
    mine = lax.dynamic_index_in_dim(value, my_bit(bit), 0, keepdims=False)
    theirs = lax.dynamic_index_in_dim(value, 1 - my_bit(bit), 0, keepdims=False)
    got = swap_bit(theirs, bit)
    return (mine.astype(f32) + got.astype(f32)).astype(value.dtype)


def pair_groups():
    count = lax.axis_size("ctx")
    return [[c for c in range(low, count, 2)] for low in range(2)]


def gather_expert(moved):
    mine = lax.all_gather(moved, "ctx", axis=0, axis_index_groups=pair_groups())
    theirs = swap_bit(mine, 0)
    low = my_bit(0) == 0
    whole = jnp.stack([jnp.where(low, mine, theirs), jnp.where(low, theirs, mine)], axis=1)
    return whole.reshape(-1, moved.shape[1])


def core_sum(grad):
    half = lax.axis_size("ctx") // 2
    value = grad.reshape(half, 2, grad.shape[0] // (2 * half), grad.shape[1])
    mine = lax.dynamic_index_in_dim(value, my_bit(0), 1, keepdims=False)
    theirs = lax.dynamic_index_in_dim(value, 1 - my_bit(0), 1, keepdims=False)
    got = swap_bit(theirs, 0)
    return (mine.astype(f32) + got.astype(f32)).astype(bf16)


class LineScatter:
    def __init__(self, halves):
        self.halves = halves
        self.size = halves[0].shape[0]
        self.place = lax.axis_index("ctx") // 2
        self.got = [[None, None] for _ in halves]

    def part(self, index, place, got):
        own = lax.dynamic_index_in_dim(
            self.halves[index], jnp.clip(place, 0, self.size - 1), 0, keepdims=False
        )
        return own if got is None else (own.astype(f32) + got.astype(f32)).astype(bf16)

    def round(self, step):
        away = self.size - 1 - step
        for index in range(len(self.halves)):
            pair = self.got[index]
            values = (
                self.part(index, self.place + away, pair[0]),
                self.part(index, self.place - away, pair[1]),
            )
            pair[0] = scatter_permute(values[0], 1, step)
            pair[1] = scatter_permute(values[1], -1, step)

    def settle(self, values):
        flat = [x for pair in self.got for x in pair]
        out = lax.optimization_barrier((*values, *flat))
        flat = out[len(values) :]
        self.got = [[flat[2 * k], flat[2 * k + 1]] for k in range(len(self.got))]
        return out[: len(values)]

    def totals(self):
        out = []
        for index, (right, left) in enumerate(self.got):
            own = lax.dynamic_index_in_dim(self.halves[index], self.place, 0, keepdims=False)
            total = own.astype(f32) + right.astype(f32) + left.astype(f32)
            out.append(turn(total.astype(bf16)))
        return out


def scatter_permute(value, step, number):
    size = lax.axis_size("ctx") // 2
    pairs = []
    for a in range(size):
        b = a + step
        if 0 <= b < size and (a <= number if step > 0 else a >= size - 1 - number):
            for low in range(2 * EXP_AXIS):
                pairs.append((a * 2 * EXP_AXIS + low, b * 2 * EXP_AXIS + low))
    return lax.ppermute(value, both, pairs)


def gelu_pair(value):
    inner = math.sqrt(2.0 / math.pi)
    square = value * value
    turned = jnp.tanh(inner * (value + 0.044715 * value * square))
    half = 0.5 * (1.0 + turned)
    slope = half + 0.5 * value * (1.0 - turned * turned) * inner * (1.0 + 3 * 0.044715 * square)
    return value * half, slope


def block_places(count, block):
    me = flat_index()
    line = count // 2
    place, low = me // (2 * EXP_AXIS), lax.rem(me, 2)
    out = []
    for k in range(line):
        for other in range(2):
            index = lax.rem(place + k, line) * 2 + (low + other * (1 - 2 * low))
            out.append(pl.ds(pl.multiple_of(index * block, block), block))
    return out


def expert_front_kernel(count, rows_ref, *refs):
    gates, ups = refs[:count], refs[count : 2 * count]
    units_ref, value_ref, slope_ref, turned = refs[2 * count :]
    block = gates[0].shape[0]

    @pl.when(pl.program_id(0) == 0)
    def _():
        for k, places in enumerate(block_places(count, block)):
            turned[:, k * block : (k + 1) * block] = rows_ref[:, places]

    rows = turned[...]
    gate = jnp.dot(rows, jnp.concatenate([r[...] for r in gates], 0), preferred_element_type=f32)
    up = jnp.dot(rows, jnp.concatenate([r[...] for r in ups], 0), preferred_element_type=f32)
    value, slope = gelu_pair(gate)
    units_ref[...] = (value * up).astype(bf16)
    value_ref[...] = value.astype(bf16)
    slope_ref[...] = (slope * up).astype(bf16)


def expert_front(rows, gates, ups):
    count, cols, tile = len(gates), gates[0].shape[1], 256
    wide = pl.BlockSpec((rows.shape[0], tile), lambda j: (0, j))
    return pl.pallas_call(
        partial(expert_front_kernel, count),
        grid=(cols // tile,),
        in_specs=[pl.BlockSpec(rows.shape, lambda j: (0, 0))]
        + [pl.BlockSpec((gates[0].shape[0], tile), lambda j: (0, j))] * (2 * count),
        out_specs=[wide] * 3,
        out_shape=[jax.ShapeDtypeStruct((rows.shape[0], cols), bf16)] * 3,
        scratch_shapes=[pltpu.VMEM(rows.shape, bf16)],
        compiler_params=pltpu.CompilerParams(vmem_limit_bytes=48 << 20),
        cost_estimate=pl.CostEstimate(
            flops=4 * rows.size * cols, bytes_accessed=4 * D * cols, transcendentals=0
        ),
        name="expert_front",
    )(rows, *gates, *ups)


def expert_middle_kernel(grads_ref, down_ref, value_ref, slope_ref, gate_ref, up_ref):
    grad = lax.dot_general(grads_ref[...], down_ref[...], last_dims, preferred_element_type=f32)
    gate_ref[...] = (grad * slope_ref[...].astype(f32)).astype(bf16)
    up_ref[...] = (grad * value_ref[...].astype(f32)).astype(bf16)


def expert_middle(grads, w_down, value, slope):
    cols, tile = w_down.shape[0], 256
    wide = pl.BlockSpec((grads.shape[0], tile), lambda j: (0, j))
    return pl.pallas_call(
        expert_middle_kernel,
        grid=(cols // tile,),
        in_specs=[
            pl.BlockSpec(grads.shape, lambda j: (0, 0)),
            pl.BlockSpec((tile, w_down.shape[1]), lambda j: (j, 0)),
            wide,
            wide,
        ],
        out_specs=[wide] * 2,
        out_shape=[jax.ShapeDtypeStruct((grads.shape[0], cols), bf16)] * 2,
        compiler_params=pltpu.CompilerParams(vmem_limit_bytes=48 << 20),
        cost_estimate=pl.CostEstimate(
            flops=2 * grads.size * cols, bytes_accessed=2 * D * cols, transcendentals=0
        ),
        name="expert_middle",
    )(grads, w_down, value, slope)


def expert_rear_kernel(count, gate_ref, up_ref, *refs):
    gates, ups = refs[:count], refs[count : 2 * count]
    out_ref, total = refs[2 * count :]
    block = gates[0].shape[0]
    weights = jnp.concatenate(
        [jnp.concatenate([r[...] for r in gates], 0), jnp.concatenate([r[...] for r in ups], 0)], 1
    )
    grads = jnp.concatenate([gate_ref[...], up_ref[...]], 1)
    term = lax.dot_general(grads, weights, last_dims, preferred_element_type=f32)

    @pl.when(pl.program_id(0) == 0)
    def _():
        total[...] = term

    @pl.when(pl.program_id(0) > 0)
    def _():
        total[...] += term

    @pl.when(pl.program_id(0) == pl.num_programs(0) - 1)
    def _():
        for k, places in enumerate(block_places(count, block)):
            out_ref[:, places] = total[:, k * block : (k + 1) * block].astype(bf16)


def expert_rear(grad_gate, grad_up, gates, ups):
    count, cols, tile = len(gates), gates[0].shape[1], 256
    wide = pl.BlockSpec((grad_gate.shape[0], tile), lambda j: (0, j))
    shape = (grad_gate.shape[0], D)
    return pl.pallas_call(
        partial(expert_rear_kernel, count),
        grid=(cols // tile,),
        in_specs=[wide] * 2
        + [pl.BlockSpec((gates[0].shape[0], tile), lambda j: (0, j))] * (2 * count),
        out_specs=pl.BlockSpec(shape, lambda j: (0, 0)),
        out_shape=jax.ShapeDtypeStruct(shape, bf16),
        scratch_shapes=[pltpu.VMEM(shape, f32)],
        compiler_params=pltpu.CompilerParams(vmem_limit_bytes=48 << 20),
        cost_estimate=pl.CostEstimate(
            flops=4 * shape[0] * D * cols, bytes_accessed=4 * D * cols, transcendentals=0
        ),
        name="expert_rear",
    )(grad_gate, grad_up, *gates, *ups)


def lane_mask(width, head, dtype):
    lane = lax.broadcasted_iota(jnp.int32, (1, width), 1)
    return ((lane // HEAD_DIM) == head).astype(dtype)


def fill_bias(ob_ref, head, bias, blocks):
    for d in range(blocks):
        first = (blocks - d - 1) * BLOCK
        window = ob_ref[0, pl.ds(head, 1), pl.ds(first, 2 * BLOCK)]
        wide = jnp.broadcast_to(window, (BLOCK, 2 * BLOCK))
        bias[d] = pltpu.roll(wide, 0, 1, stride=1, stride_axis=0)[:, BLOCK:]


def transposed(value):
    return value.astype(f32).T.astype(bf16)


def attend_kernel(blocks, heads, qkv_ref, ob_ref, att_ref, summed_ref, total_ref, bias, kt):
    width = qkv_ref.shape[2]
    for head in range(heads):
        fill_bias(ob_ref, head, bias.at[head], blocks)
    keep = [lane_mask(width, head, f32) for head in range(heads)]
    row = lax.broadcasted_iota(jnp.int32, (width, 1), 0) // HEAD_DIM
    for kb in range(blocks):
        cols = slice(kb * BLOCK, (kb + 1) * BLOCK)
        turned = transposed(qkv_ref[1, cols, :])
        for head in range(heads):
            kt[head, :, cols] = turned * (row == head).astype(bf16)

    for qb in range(blocks):
        rows = slice(qb * BLOCK, (qb + 1) * BLOCK)
        queries = qkv_ref[0, rows, :] * jnp.asarray(score_scale, bf16)

        def step(kb, carry):
            cols = pl.ds(pl.multiple_of(kb * BLOCK, BLOCK), BLOCK)
            values = qkv_ref[2, cols, :]
            out = []
            for head in range(heads):
                tot, acc = carry[head]
                score = jnp.dot(queries, kt[head, :, cols], preferred_element_type=f32)
                expo = jnp.exp(score + bias[head, qb - kb])
                tot = tot + (expo[:, :128] + expo[:, 128:])
                acc = acc + jnp.dot(expo.astype(bf16), values, preferred_element_type=f32)
                out.append((tot, acc))
            return tuple(out)

        carry = tuple(
            (jnp.zeros((BLOCK, 128), f32), jnp.zeros((BLOCK, width), f32)) for _ in range(heads)
        )
        for kb in range(qb + 1):
            carry = step(kb, carry)
        summed = sum(carry[head][1] * keep[head] for head in range(heads))
        total = sum(
            jnp.sum(carry[head][0], axis=1, keepdims=True) * keep[head] for head in range(heads)
        )
        summed_ref[rows, :] = summed
        total_ref[rows, :] = total
        att_ref[rows, :] = (summed / total).astype(bf16)


def attend(qkv, ob):
    _, length, width = qkv.shape
    lanes = min(width, 128)
    heads = lanes // HEAD_DIM
    steps = width // lanes
    blocks = length // BLOCK
    rows = pl.BlockSpec((length, lanes), lambda i: (0, i))
    return pl.pallas_call(
        partial(attend_kernel, blocks, heads),
        grid=(steps,),
        in_specs=[
            pl.BlockSpec((3, length, lanes), lambda i: (0, 0, i)),
            pl.BlockSpec((1, heads, 2 * length), lambda i: (i, 0, 0)),
        ],
        out_specs=[rows, rows, rows],
        out_shape=[
            jax.ShapeDtypeStruct((length, width), bf16),
            jax.ShapeDtypeStruct((length, width), f32),
            jax.ShapeDtypeStruct((length, width), f32),
        ],
        scratch_shapes=[
            pltpu.VMEM((heads, blocks, BLOCK, BLOCK), f32),
            pltpu.VMEM((heads, lanes, length), bf16),
        ],
        compiler_params=pltpu.CompilerParams(vmem_limit_bytes=48 << 20),
        cost_estimate=pl.CostEstimate(
            flops=4 * length * length * width, bytes_accessed=20 * length * width, transcendentals=0
        ),
        name="attend",
    )(qkv, ob.reshape(steps, heads, 2 * length))


def attend_back_kernel(
    blocks, heads, qkv_ref, ob_ref, da_ref, summed_ref, total_ref, dqkv_ref, diag_ref,
    bias, diff, qt, kt, km, vt, dm, dmt, dt, acc_k, acc_v,
):
    width = qkv_ref.shape[2]
    lanes = [slice(head * HEAD_DIM, (head + 1) * HEAD_DIM) for head in range(heads)]
    for head in range(heads):
        fill_bias(ob_ref, head, bias.at[head], blocks)
    diff[...] = jnp.zeros_like(diff)
    acc_k[...] = jnp.zeros_like(acc_k)
    acc_v[...] = jnp.zeros_like(acc_v)
    row = lax.broadcasted_iota(jnp.int32, (width, 1), 0) // HEAD_DIM
    scale = jnp.asarray(score_scale, bf16)
    for b in range(blocks):
        rows = slice(b * BLOCK, (b + 1) * BLOCK)
        qt[:, rows] = transposed(qkv_ref[0, rows, :]) * scale
        turned = transposed(qkv_ref[1, rows, :])
        vt[:, rows] = transposed(qkv_ref[2, rows, :])
        grad = da_ref[rows, :].astype(f32)
        total = total_ref[rows, :]
        scaled = grad / total
        dmt[:, rows] = transposed(scaled)
        inner = scaled * summed_ref[rows, :] / total
        for head in range(heads):
            mask = lane_mask(width, head, f32)
            kt[head, :, rows] = turned * (row == head).astype(bf16)
            km[head, rows, :] = qkv_ref[1, rows, :] * lane_mask(width, head, bf16)
            dm[head, rows, :] = (scaled * mask).astype(bf16)
            shift = -jnp.sum(inner * mask, axis=1, keepdims=True)
            dt[head, rows, :] = jnp.broadcast_to(shift, (BLOCK, 128))

    for qb in range(blocks):
        rows = slice(qb * BLOCK, (qb + 1) * BLOCK)
        queries = qkv_ref[0, rows, :] * scale
        shifts = [dt[head, rows, :] for head in range(heads)]

        def step(kb, acc_q):
            cols = pl.ds(pl.multiple_of(kb * BLOCK, BLOCK), BLOCK)
            for head in range(heads):
                score = jnp.dot(queries, kt[head, :, cols], preferred_element_type=f32)
                expo = jnp.exp(score + bias[head, qb - kb])
                probs = jnp.dot(dm[head, rows, :], vt[:, cols], preferred_element_type=f32)
                shift = jnp.concatenate([shifts[head]] * (BLOCK // 128), axis=1)
                dscore = (expo * (probs + shift)).astype(bf16)
                diff[head, qb - kb] += dscore.astype(f32)
                acc_q = acc_q + jnp.dot(dscore, km[head, cols, :], preferred_element_type=f32)
                acc_k[lanes[head], cols] += jnp.dot(
                    qt[lanes[head], rows], dscore, preferred_element_type=f32
                )
                acc_v[lanes[head], cols] += jnp.dot(
                    dmt[lanes[head], rows], expo.astype(bf16), preferred_element_type=f32
                )
            return acc_q

        acc_q = jnp.zeros((BLOCK, width), f32)
        for kb in range(qb + 1):
            acc_q = step(kb, acc_q)
        dqkv_ref[0, rows, :] = (acc_q * score_scale).astype(bf16)

    lower = lax.broadcasted_iota(jnp.int32, (8, 2 * BLOCK), 0)
    for head in range(heads):
        for d in range(blocks):

            def add_rows(i, fold):
                part = diff[head, d, pl.ds(pl.multiple_of(i * 8, 8), 8), :]
                wide = jnp.concatenate([jnp.zeros((8, BLOCK), f32), part], axis=1)
                return fold + pltpu.roll(wide, 2 * BLOCK - 8 * i, 1)

            fold = lax.fori_loop(
                0, BLOCK // 8, add_rows, jnp.zeros((8, 2 * BLOCK), f32), unroll=8
            )
            for bit in (1, 2, 4):
                fold = jnp.where((lower & bit) != 0, pltpu.roll(fold, 2 * BLOCK - bit, 1), fold)
            diag_ref[0, pl.ds(head * blocks + d, 1), :] = jnp.sum(fold, axis=0, keepdims=True)
    for b in range(blocks):
        rows = slice(b * BLOCK, (b + 1) * BLOCK)
        dqkv_ref[1, rows, :] = acc_k[:, rows].T.astype(bf16)
        dqkv_ref[2, rows, :] = acc_v[:, rows].T.astype(bf16)


def attend_back(qkv, ob, grad, summed, total):
    _, length, width = qkv.shape
    lanes = min(width, 128)
    heads = lanes // HEAD_DIM
    steps = width // lanes
    blocks = length // BLOCK
    rows = pl.BlockSpec((length, lanes), lambda i: (0, i))
    wide = pl.BlockSpec((3, length, lanes), lambda i: (0, 0, i))
    dqkv, diag = pl.pallas_call(
        partial(attend_back_kernel, blocks, heads),
        grid=(steps,),
        in_specs=[wide, pl.BlockSpec((1, heads, 2 * length), lambda i: (i, 0, 0)), rows, rows, rows],
        out_specs=[wide, pl.BlockSpec((1, heads * blocks, 2 * BLOCK), lambda i: (i, 0, 0))],
        out_shape=[
            jax.ShapeDtypeStruct((3, length, width), bf16),
            jax.ShapeDtypeStruct((steps, heads * blocks, 2 * BLOCK), f32),
        ],
        scratch_shapes=[
            pltpu.VMEM((heads, blocks, BLOCK, BLOCK), f32),
            pltpu.VMEM((heads, blocks, BLOCK, BLOCK), f32),
            pltpu.VMEM((lanes, length), bf16),
            pltpu.VMEM((heads, lanes, length), bf16),
            pltpu.VMEM((heads, length, lanes), bf16),
            pltpu.VMEM((lanes, length), bf16),
            pltpu.VMEM((heads, length, lanes), bf16),
            pltpu.VMEM((lanes, length), bf16),
            pltpu.VMEM((heads, length, 128), f32),
            pltpu.VMEM((lanes, length), f32),
            pltpu.VMEM((lanes, length), f32),
        ],
        compiler_params=pltpu.CompilerParams(vmem_limit_bytes=56 << 20),
        cost_estimate=pl.CostEstimate(
            flops=10 * length * length * width, bytes_accessed=30 * length * width, transcendentals=0
        ),
        name="attend_back",
    )(qkv, ob.reshape(steps, heads, 2 * length), grad, summed, total)
    return dqkv, diag.reshape(steps * heads, blocks, 2 * BLOCK)


def norm_back(norm_input, factor, gain_wide, grad_normed):
    scaled = grad_normed * gain_wide
    gain_grad = jnp.sum(grad_normed * norm_input * factor, axis=0)
    mean_term = jnp.mean(scaled * norm_input, axis=-1, keepdims=True)
    return (factor * scaled - norm_input * factor * factor * factor * mean_term, gain_grad)


def adamw_step(master, gradient, first_old, second_old):
    first_new = decay_rate * first_old + (1.0 - decay_rate) * gradient
    second_new = decay_rate * second_old + (1.0 - decay_rate) * gradient * gradient
    correct = 1.0 - decay_rate**STEP
    update = -learn_rate * (
        first_new / correct / (jnp.sqrt(second_new / correct) + eps_adam) + weight_decay * master
    )
    return (gradient, first_new, second_new, update)


def layer(tokens, cotangent, bucket_ids, routes, *state):
    masters, firsts, seconds = state[:9], state[9:18], state[18:]
    (
        qkv_master, out_master, router_master, gain_attn_master, gain_mix_master, table_master,
        gate_master, up_master, down_master,
    ) = masters
    micro, tok_rows = tokens.shape[0], tokens.shape[2]
    cycle = lax.axis_size("ctx")
    count = cycle * EXP_AXIS
    length = tok_rows * cycle
    group = cycle // micro
    width = D // group
    place = lax.axis_index("ctx")
    head_group = place % group
    line = cycle // 2
    line_place = place // 2
    rows = D // count
    experts_all = router_master.shape[1]
    capacity = 5 * tok_rows * TOP // (4 * experts_all)
    low = my_bit(0) == 0

    tok = tokens[:, 0]
    cols = qkv_master.astype(bf16).reshape(3 * rows, group, width).transpose(1, 0, 2)
    small = jnp.concatenate(
        [
            router_master.reshape(-1), gain_attn_master, gain_mix_master, table_master,
        ]
    ).astype(bf16)
    small_size = small.shape[0]
    small = jnp.pad(small, (0, 16 * width - small_size)).reshape(1, 16, width)
    cols = jnp.concatenate([cols, jnp.broadcast_to(small, (group, 16, width))], axis=1)
    w_out = lax.all_gather(out_master.astype(bf16), both, axis=0, tiled=True)
    gate_own, up_own, down_own = (
        turn(member[0].astype(bf16)) for member in (gate_master, up_master, down_master)
    )
    seq, gathered = opening(tok, cols)
    gate_own, up_own, seq, gathered = lax.optimization_barrier((gate_own, up_own, seq, gathered))
    lines = [[own, own] for own in (gate_own, up_own)]
    right, left = [], []

    def line_round(step):
        for pair in lines:
            pair[0] = line_permute(pair[0], 1, step)
            pair[1] = line_permute(pair[1], -1, step)
        right.append([pair[0] for pair in lines])
        left.append([pair[1] for pair in lines])

    def line_settle(value):
        flat = lax.optimization_barrier((value, *[x for pair in lines for x in pair]))
        lines[0][0], lines[0][1], lines[1][0], lines[1][1] = flat[1:]
        right[-1], left[-1] = [flat[1], flat[3]], [flat[2], flat[4]]
        return flat[0]

    line_round(0)
    seq = seq.reshape(length, D)
    w_qkv = gathered[:, :, : 3 * rows].reshape(EXP_AXIS, cycle, 3, rows, width)
    w_qkv = w_qkv.transpose(2, 1, 0, 3, 4).reshape(3, D, width)
    small = gathered[:, :, 3 * rows :].reshape(EXP_AXIS, cycle, 16 * width)[:, :, :small_size]
    small = small.transpose(1, 0, 2).reshape(count, small_size)
    edges = (0, rows * experts_all, rows * (experts_all + 1), rows * (experts_all + 2))
    router_bf = small[:, : edges[1]].reshape(D, experts_all)
    gain_attn = small[:, edges[1] : edges[2]].reshape(D).astype(f32)
    gain_mix = small[:, edges[2] : edges[3]].reshape(D).astype(f32)
    table = small[:, edges[3] :].reshape(HEADS, -1)
    bucket_count = table.shape[1]
    router_wide = router_bf.astype(f32)
    bucket_hits = bucket_ids[:, None] == jnp.arange(bucket_count, dtype=jnp.int32)[None, :]
    own_heads = HEADS // group
    own_table = lax.dynamic_slice_in_dim(table, head_group * own_heads, own_heads, 0)
    offset_bias = lax.dot_general(
        own_table, bucket_hits.astype(bf16), last_dims, preferred_element_type=f32
    )
    offset_bias = jnp.pad(offset_bias, ((0, 0), (1, 0)))[:, :-1]

    seq_wide = seq.astype(f32)
    seq_factor = lax.rsqrt(jnp.mean(seq_wide * seq_wide, axis=-1, keepdims=True) + eps_norm)
    normed = (seq_wide * seq_factor * gain_attn).astype(bf16)
    qkv = jnp.einsum("td,cde->cte", normed, w_qkv, preferred_element_type=f32).astype(bf16)
    attended, summed, total = attend(qkv, offset_bias)

    attended = line_settle(attended)
    back = cycle_swap(attended.reshape(cycle, tok_rows, width), 1)
    back, down_own = lax.optimization_barrier((line_settle(back), down_own))
    line_round(1)
    toks = micro * tok_rows
    attended_bf = back.reshape(micro, group, tok_rows, width).transpose(0, 2, 1, 3)
    attended_bf = attended_bf.reshape(toks, D)
    inputs = tok.reshape(toks, D).astype(f32)
    factor_attn = lax.rsqrt(jnp.mean(inputs * inputs, axis=-1, keepdims=True) + eps_norm)
    hidden_state = inputs + jnp.dot(attended_bf, w_out, preferred_element_type=f32)
    factor_mix = lax.rsqrt(jnp.mean(hidden_state * hidden_state, axis=-1, keepdims=True) + eps_norm)
    normed_mix = hidden_state * factor_mix * gain_mix
    normed_bf = normed_mix.astype(bf16)
    logits = jnp.dot(normed_bf, router_bf, preferred_element_type=f32)
    router_probs = jax.nn.softmax(logits, axis=-1)
    route_rows = routes.reshape(micro, tok_rows, TOP)
    expert_ids = jnp.arange(experts_all, dtype=jnp.int32)
    picked = (route_rows.reshape(toks, TOP)[:, :, None] == expert_ids).astype(f32)
    chosen = jnp.sum(picked * router_probs[:, None, :], axis=-1)
    chosen_sum = jnp.sum(chosen, axis=-1, keepdims=True)
    gate_share = chosen / chosen_sum
    flat_routes = route_rows.reshape(micro, tok_rows * TOP)
    route_hits = (flat_routes[:, :, None] == expert_ids).astype(jnp.int32)
    before = jnp.cumsum(route_hits, axis=1) - route_hits
    micro_ids = jnp.arange(micro, dtype=jnp.int32)[:, None]
    slot_index = (flat_routes * micro + micro_ids) * capacity + jnp.sum(before * route_hits, axis=-1)
    slot_index = slot_index.reshape(toks, TOP)
    slot_count = experts_all * micro * capacity
    slot_ids = jnp.arange(slot_count, dtype=jnp.int32)
    hits = [(slot_index[:, choice, None] == slot_ids).astype(bf16) for choice in range(TOP)]
    slots = (experts_all, micro, capacity, D)
    sent_rows = lax.dot_general(sum(hits), normed_bf, first_dims, preferred_element_type=f32)
    dy_rows = cotangent.reshape(toks, D).astype(f32)
    scaled_dy = [
        (gate_share[:, choice, None] * dy_rows).astype(bf16) for choice in range(TOP)
    ]
    sent_grads = lax.dot_general(
        jnp.concatenate(hits, axis=0), jnp.concatenate(scaled_dy, axis=0), first_dims,
        preferred_element_type=f32,
    )
    sent_rows = line_settle(sent_rows.astype(bf16))
    if line > 3:
        line_round(2)
    got_rows, got_grads = plane_swap(
        (sent_rows.reshape(slots), sent_grads.astype(bf16).reshape(slots)), True, 2
    )
    for step in range(3, line - 1):
        line_round(step)
    flat_rows = got_rows.reshape(-1, D)
    flat_grads = got_grads.reshape(-1, D)

    def blocks_of(index, own):
        blocks = [own] + [
            jnp.where(line_place + k < line, left[k - 1][index], right[line - 1 - k][index])
            for k in range(1, line)
        ]
        return [block for mine in blocks for block in (mine, swap_bit(mine, 0))]

    gates, ups = blocks_of(0, gate_own), blocks_of(1, up_own)
    w_down = gather_expert(down_own)
    kernels = gate_own.shape[0] % 128 == 0
    if kernels:
        units, value, slope = expert_front(flat_rows, gates, ups)
    else:

        def whole(blocks):
            pieces = []
            for mine, theirs in zip(blocks[::2], blocks[1::2]):
                pieces += [jnp.where(low, mine, theirs), jnp.where(low, theirs, mine)]
            return jnp.concatenate(pieces, axis=0)

        def turned(value, shift):
            twice = jnp.concatenate([value, value], axis=1)
            return lax.dynamic_slice_in_dim(twice, shift * (D // line), D, 1)

        w_gate, w_up = whole(gates), whole(ups)
        turned_rows = turned(flat_rows, line_place)
        gate_pre = jnp.dot(turned_rows, w_gate, preferred_element_type=f32)
        up_pre = jnp.dot(turned_rows, w_up, preferred_element_type=f32)
        value, slope = gelu_pair(gate_pre)
        units, slope = (value * up_pre).astype(bf16), slope * up_pre
    down_grad = lax.dot_general(units, flat_grads, first_dims, preferred_element_type=f32)
    down_line = LineScatter([core_sum(down_grad.astype(bf16))])
    down_line.round(0)
    grad_gate, grad_up = expert_middle(flat_grads, w_down, value, slope)
    (grad_up,) = down_line.settle((grad_up,))
    down_line.round(1)
    up_grad = lax.dot_general(flat_rows, grad_up, first_dims, preferred_element_type=f32)
    gate_grad = lax.dot_general(flat_rows, grad_gate, first_dims, preferred_element_type=f32)
    both_line = LineScatter([core_sum(up_grad.astype(bf16)), core_sum(gate_grad.astype(bf16))])
    (grad_gate,) = down_line.settle((grad_gate,))
    for step in range(2, line - 1):
        down_line.round(step)
    both_line.round(0)
    out_rows = jnp.dot(units, w_down, preferred_element_type=f32).astype(bf16)
    if kernels:
        grad_rows = expert_rear(grad_gate, grad_up, gates, ups)
    else:
        grad_rows = lax.dot_general(grad_gate, w_gate, last_dims, preferred_element_type=f32)
        grad_rows = grad_rows + lax.dot_general(
            grad_up, w_up, last_dims, preferred_element_type=f32
        )
        grad_rows = turned(grad_rows.astype(bf16), line - line_place)
    back_out, back_grad = plane_swap((out_rows.reshape(slots), grad_rows.reshape(slots)), False, 3)
    back_out, back_grad = both_line.settle((back_out, back_grad))
    both_line.round(1)
    back_out, back_grad = back_out.reshape(slot_count, D), back_grad.reshape(slot_count, D)

    returned = [jnp.dot(hit, back_out, preferred_element_type=f32) for hit in hits]
    mix_out = sum(gate_share[:, c, None] * returned[c] for c in range(TOP))
    output = (hidden_state + mix_out).astype(bf16)
    grad_gates = jnp.stack([jnp.sum(dy_rows * returned[c], axis=-1) for c in range(TOP)], axis=1)
    grad_chosen = grad_gates / chosen_sum - jnp.sum(grad_gates * chosen, axis=-1, keepdims=True) / (
        chosen_sum * chosen_sum
    )
    grad_probs = jnp.sum(grad_chosen[:, :, None] * picked, axis=1)
    grad_logits = router_probs * (
        grad_probs - jnp.sum(router_probs * grad_probs, axis=-1, keepdims=True)
    )
    router_grad = lax.dot_general(
        normed_bf.astype(f32), grad_logits, first_dims, precision=highest
    )
    grad_normed = jnp.dot(sum(hits), back_grad, preferred_element_type=f32) + lax.dot_general(
        grad_logits, router_wide, last_dims, precision=highest
    )
    grad_hidden, gain_mix_grad = norm_back(hidden_state, factor_mix, gain_mix, grad_normed)
    grad_hidden = grad_hidden + dy_rows
    grad_branch = grad_hidden.astype(bf16)
    grad_attended = lax.dot_general(grad_branch, w_out, last_dims, preferred_element_type=f32)
    grad_attended = grad_attended.astype(bf16).reshape(micro, tok_rows, group, width)
    grad_attended = grad_attended.transpose(0, 2, 1, 3).reshape(cycle, tok_rows, width)
    (grad_attended,) = both_line.settle((grad_attended,))
    grad_attended = cycle_swap(grad_attended, 4).reshape(length, width)
    for step in range(2, line - 1):
        both_line.round(step)
    out_grad = lax.dot_general(attended_bf, grad_branch, first_dims, preferred_element_type=f32)
    out_grad = out_grad.astype(bf16).reshape(cycle, 2, 2, rows, D).transpose(2, 1, 0, 3, 4)
    out_grad = cube_sum(out_grad, 0)
    out_grad = cube_sum(out_grad, 1)

    dqkv, diag = attend_back(qkv, offset_bias, grad_attended, summed, total)
    qkv_grad = jnp.einsum("td,cte->cde", normed, dqkv, preferred_element_type=f32)
    qkv_grad = qkv_grad.astype(bf16).reshape(3, cycle, 2, 2, rows, width)
    qkv_grad = qkv_grad.transpose(3, 2, 1, 0, 4, 5)
    qkv_grad = cube_sum(qkv_grad, 0)
    qkv_grad = cube_sum(qkv_grad, 1)
    partial_normed = jnp.einsum("cte,cde->td", dqkv, w_qkv, preferred_element_type=f32)
    (partial_normed,) = both_line.settle((partial_normed.astype(bf16),))
    partial_normed = partial_normed.reshape(cycle, tok_rows, D)
    pieces = cycle_swap(partial_normed, 5)
    grad_normed_attn = jnp.sum(pieces.reshape(micro, group, tok_rows, D).astype(f32), axis=1)
    grad_inputs, gain_attn_grad = norm_back(
        inputs, factor_attn, gain_attn, grad_normed_attn.reshape(toks, D)
    )
    grad_inputs = grad_inputs + grad_hidden

    (down_sum,) = down_line.totals()
    up_sum, gate_sum = both_line.totals()
    blocks = length // BLOCK
    offset_grad = jnp.zeros((own_heads, 2 * length), f32)
    for d in range(blocks):
        first = (blocks - d - 1) * BLOCK
        offset_grad = offset_grad + jnp.pad(
            diag[:, d], ((0, 0), (first, 2 * length - first - 2 * BLOCK))
        )
    offset_grad = jnp.pad(offset_grad[:, 1:], ((0, 0), (0, 1)))
    own_grad = jnp.dot(offset_grad, bucket_hits.astype(f32), precision=highest)
    table_grad = lax.dynamic_update_slice_in_dim(
        jnp.zeros((HEADS, bucket_count), f32), own_grad, head_group * own_heads, 0
    )
    small_grads = jnp.concatenate(
        [
            router_grad.reshape(count, -1), gain_attn_grad.reshape(count, -1),
            gain_mix_grad.reshape(count, -1), table_grad.reshape(count, -1),
        ],
        axis=1,
    )
    small_grads = jnp.pad(small_grads, ((0, 0), (0, -small_grads.shape[1] % 128)))
    qkv_grad, out_grad, small_parts = closing(qkv_grad, out_grad, small_grads[:, None])
    qkv_sum = jnp.sum(qkv_grad.reshape(micro, group, 3, rows, width).astype(f32), axis=0)
    qkv_sum = qkv_sum.transpose(1, 2, 0, 3).reshape(3, rows, D)
    out_sum = jnp.sum(out_grad.astype(f32), axis=0)
    small_sum = jnp.sum(small_parts[:, 0], axis=0)[:small_size]
    gradients = (
        qkv_sum,
        out_sum,
        small_sum[: edges[1]].reshape(rows, experts_all),
        small_sum[edges[1] : edges[2]],
        small_sum[edges[2] : edges[3]],
        small_sum[edges[3] :],
        *(total[None].astype(f32) for total in (gate_sum, up_sum, down_sum)),
    )
    results = [
        adamw_step(master, gradient, first_old, second_old)
        for master, gradient, first_old, second_old in zip(masters, gradients, firsts, seconds)
    ]
    flat = [result[kind] for kind in range(4) for result in results]
    return (output.reshape(tokens.shape), grad_inputs.reshape(tokens.shape), *flat)


def solution(mesh):
    token_spec = P(None, "exp", "ctx", None)
    weight_specs = (
        P(None, both, None), P(both, None), P(both, None), P(both), P(both), P(both),
        P("exp", "ctx", None), P("exp", "ctx", None), P("exp", "ctx", None),
    )
    return jax.shard_map(
        layer,
        mesh=mesh,
        in_specs=(token_spec, token_spec, P(), token_spec) + weight_specs * 3,
        out_specs=(token_spec, token_spec) + weight_specs * 4,
        check_vma=False,
    )
```

profile of v0, /device:TPU:5, one launch (start us, length us, event | category | flops | bytes accessed | tf_op | source)
XLA Modules:
  0.0 755.3 jit_solution(4279331198604499386)
XLA Ops:
  27.2 53.6 %shard_map.590 = (bf16[8,128,1024]{2,1,0:T(8,128)(2,1)S(1)}, bf16[4,8,112,256]{3,2,1,0:T(8,128)(2,1)S(1)}) custom-call(bf16[2,128,1024]{2,1,0:T(8,128)(2,1)S(1)} %bitcast.335, bf16[4,112,256]{2,1,0:T(8,128)(2,1)S(1)} %pad_maximum_fusion.1.col_ref), custom_call_target="tpu_custom_call" | custom-call | bytes 6029312 | tf_op jit(solution)/shard_map/pallas_call | solution.py:79
  124.5 14.2 %shard_map.591 = bf16[8,128,256]{2,1,0:T(8,128)(2,1)S(1)} custom-call(bf16[8,128,256]{2,1,0:T(8,128)(2,1)S(1)} %bitcast.349), custom_call_target="tpu_custom_call" | custom-call | bytes 4194304 | tf_op jit(solution)/shard_map/pallas_call | solution.py:79
  150.5 11.0 %collective-permute-done.8 = bf16[128,2816]{1,0:T(8,128)(2,1)} collective-permute-done((bf16[128,2816]{1,0:T(8,128)(2,1)}, bf16[128,2816]{1,0:T(8,128)(2,1)}, u32[]{:S(2)}, u32[]{:S(2)}) %collective-permute-start.8) | collective-permute-done | bytes 720928 | tf_op jit(solution)/shard_map/ppermute | solution.py:281
  161.6 33.0 %collective-permute-done.10 = bf16[128,2816]{1,0:T(8,128)(2,1)} collective-permute-done((bf16[128,2816]{1,0:T(8,128)(2,1)}, bf16[128,2816]{1,0:T(8,128)(2,1)}, u32[]{:S(2)}, u32[]{:S(2)}) %collective-permute-start.10) | collective-permute-done | bytes 720928 | tf_op jit(solution)/shard_map/ppermute | solution.py:281
  202.3 8.8 %collective-permute-start.20 = (bf16[128,2816]{1,0:T(8,128)(2,1)S(1)}, bf16[128,2816]{1,0:T(8,128)(2,1)S(1)}, u32[]{:S(2)}, u32[]{:S(2)}) collective-permute-start(bf16[128,2816]{1,0:T(8,128)(2,1)S(1)} %broadcast_select_fusion.2.refs_12_), channel_id=1, source_target_pairs={{0,1},{1,0},{2,3},{3,2},{4,5},{5,4},{6,7},{7,6},{8,9},{9,8},{10,11... | collective-permute-start | bytes 2162696 | tf_op jit(solution)/shard_map/ppermute | solution.py:36
  212.3 26.7 %collective-permute-done.15 = bf16[128,2816]{1,0:T(8,128)(2,1)S(1)} collective-permute-done((bf16[128,2816]{1,0:T(8,128)(2,1)}, bf16[128,2816]{1,0:T(8,128)(2,1)S(1)}, u32[]{:S(2)}, u32[]{:S(2)}) %collective-permute-start.15) | collective-permute-done | bytes 720928 | tf_op jit(solution)/shard_map/ppermute | solution.py:281
  242.8 11.6 %collective-permute-done.21 = bf16[128,2816]{1,0:T(8,128)(2,1)S(1)} collective-permute-done((bf16[128,2816]{1,0:T(8,128)(2,1)}, bf16[128,2816]{1,0:T(8,128)(2,1)S(1)}, u32[]{:S(2)}, u32[]{:S(2)}) %collective-permute-start.21) | collective-permute-done | bytes 720928 | tf_op jit(solution)/shard_map/ppermute | solution.py:281
  259.2 31.9 %shard_map.592 = (bf16[4,2,80,1024]{3,2,1,0:T(8,128)(2,1)S(1)}, bf16[4,2,80,1024]{3,2,1,0:T(8,128)(2,1)S(1)}) custom-call(bf16[4,2,80,1024]{3,2,1,0:T(8,128)(2,1)S(1)} %bitcast.345, bf16[4,2,80,1024]{3,2,1,0:T(8,128)(2,1)S(1)} %bitcast.348), custom_call_target="tpu_custom_call" | custom-call | bytes 20971520 | tf_op jit(solution)/shard_map/pallas_call | solution.py:79
  293.4 17.7 %expert_front.1 = (bf16[640,2816]{1,0:T(8,128)(2,1)}, bf16[640,2816]{1,0:T(8,128)(2,1)}, bf16[640,2816]{1,0:T(8,128)(2,1)}) custom-call(bf16[640,1024]{1,0:T(8,128)(2,1)} %bitcast.352, bf16[128,2816]{1,0:T(8,128)(2,1)} %broadcast_select_fusion.11.refs_0_, bf16[128,2816]{1,0:T(8,128)(2,1)} %collective-permute-done.11.refs_1_, ...), custom_call_target="tpu_custom_call" | custom-call | flops 7381975040 | bytes 11534336 | tf_op jit(solution)/shard_map/expert_front/pallas_call | solution.py:407
  311.2 7.0 convolution_convert_fusion.2
  343.1 12.5 %expert_middle.1 = (bf16[640,2816]{1,0:T(8,128)(2,1)S(1)}, bf16[640,2816]{1,0:T(8,128)(2,1)}) custom-call(bf16[640,1024]{1,0:T(8,128)(2,1)S(1)} %bitcast.343, bf16[2816,1024]{1,0:T(8,128)(2,1)} %bitcast.355, bf16[640,2816]{1,0:T(8,128)(2,1)} %get-tuple-element.127.value_ref, bf16[640,2816]{1,0:T(8,128)(2,1)} %get-tuple-element.128.slope_ref), custom_call_target="tpu_custom_call" | custom-call | flops 3690987520 | bytes 5767168 | tf_op jit(solution)/shard_map/expert_middle/pallas_call | solution.py:432
  378.1 7.0 collective-permute-done.27
  397.4 16.0 %expert_rear.1 = bf16[640,1024]{1,0:T(8,128)(2,1)} custom-call(bf16[640,2816]{1,0:T(8,128)(2,1)} %copy-done.10, bf16[640,2816]{1,0:T(8,128)(2,1)} %get-tuple-element.134.up_ref, bf16[128,2816]{1,0:T(8,128)(2,1)} %broadcast_select_fusion.11.refs_0_, bf16[128,2816]{1,0:T(8,128)(2,1)} %collective-permute-done.11.refs_1_, bf16[128,2816]{1,0:T(8,128)(2,1)S(1)} %copy-done.5, ...), custom_call_target="tpu_custom_call" | custom-call | flops 7381975040 | bytes 11534336 | tf_op jit(solution)/shard_map/expert_rear/pallas_call | solution.py:479
  414.7 33.0 %shard_map.593 = (bf16[4,2,80,1024]{3,2,1,0:T(8,128)(2,1)S(1)}, bf16[4,2,80,1024]{3,2,1,0:T(8,128)(2,1)S(1)}) custom-call(bf16[4,2,80,1024]{3,2,1,0:T(8,128)(2,1)S(1)} %bitcast.346, bf16[4,2,80,1024]{3,2,1,0:T(8,128)(2,1)S(1)} %bitcast.347), custom_call_target="tpu_custom_call" | custom-call | bytes 20971520 | tf_op jit(solution)/shard_map/pallas_call | solution.py:79
  477.8 13.3 %collective-permute-done.30 = bf16[128,2816]{1,0:T(8,128)(2,1)S(1)} collective-permute-done((bf16[128,2816]{1,0:T(8,128)(2,1)S(1)}, bf16[128,2816]{1,0:T(8,128)(2,1)S(1)}, u32[]{:S(2)}, u32[]{:S(2)}) %collective-permute-start.30) | collective-permute-done | bytes 720928 | tf_op jit(solution)/shard_map/ppermute | solution.py:361
  523.3 14.4 %collective-permute-done.37 = bf16[128,2816]{1,0:T(8,128)(2,1)} collective-permute-done((bf16[128,2816]{1,0:T(8,128)(2,1)}, bf16[128,2816]{1,0:T(8,128)(2,1)}, u32[]{:S(2)}, u32[]{:S(2)}) %collective-permute-start.37) | collective-permute-done | bytes 720928 | tf_op jit(solution)/shard_map/ppermute | solution.py:361
  537.7 15.5 %shard_map.594 = bf16[8,128,256]{2,1,0:T(8,128)(2,1)S(1)} custom-call(bf16[8,128,256]{2,1,0:T(8,128)(2,1)S(1)} %bitcast.340), custom_call_target="tpu_custom_call" | custom-call | bytes 4194304 | tf_op jit(solution)/shard_map/pallas_call | solution.py:79
  554.1 25.3 %attend_back.1 = (bf16[3,1024,256]{2,1,0:T(8,128)(2,1)}, f32[2,8,512]{2,1,0:T(8,128)}) custom-call(bf16[3,1024,256]{2,1,0:T(8,128)(2,1)} %copy-done.19, f32[2,2,2048]{2,1,0:T(2,128)} %copy-done.9, bf16[1024,256]{1,0:T(8,128)(2,1)} %bitcast.350, f32[1024,256]{1,0:T(8,128)} %copy-done.20, f32[1024,256]{1,0:T(8,128)} %copy-done.21), custom_call_target="tpu_custom_call" | custom-call | flops 2684354560 | bytes 7864320 | tf_op jit(solution)/shard_map/attend_back/pallas_call | solution.py:675
  595.3 5.2 collective-permute-start.39
  615.0 14.3 %collective-permute-done.42 = bf16[128,2816]{1,0:T(8,128)(2,1)S(1)} collective-permute-done((bf16[128,2816]{1,0:T(8,128)(2,1)S(1)}, bf16[128,2816]{1,0:T(8,128)(2,1)S(1)}, u32[]{:S(2)}, u32[]{:S(2)}) %collective-permute-start.42) | collective-permute-done | bytes 720928 | tf_op jit(solution)/shard_map/ppermute | solution.py:361
  631.3 37.9 %shard_map.595 = bf16[8,128,1024]{2,1,0:T(8,128)(2,1)S(1)} custom-call(bf16[8,128,1024]{2,1,0:T(8,128)(2,1)S(1)} %bitcast.339), custom_call_target="tpu_custom_call" | custom-call | bytes 16777216 | tf_op jit(solution)/shard_map/pallas_call | solution.py:79
  670.4 7.2 collective-permute-start.47
  686.3 6.7 collective-permute-done.44
  693.1 39.4 %shard_map.596 = (bf16[8,3,32,256]{3,2,1,0:T(8,128)(2,1)S(1)}, bf16[8,32,1024]{2,1,0:T(8,128)(2,1)S(1)}, f32[32,1,256]{2,1,0:T(1,128)S(1)}) custom-call(bf16[8,3,32,256]{3,2,1,0:T(8,128)(2,1)S(1)} %fusion.64.col_ref, bf16[8,32,1024]{2,1,0:T(8,128)(2,1)S(1)} %fusion.56.out_in, f32[32,1,256]{2,1,0:T(1,128)S(1)} %broadcast_in_dim.11.small_ref), custom_call_target="tpu_custom_call" | custom-call | bytes 7602176 | tf_op jit(solution)/shard_map/pallas_call | solution.py:79
  (518 shorter events, 275.6 us)
Async XLA Ops:
  7.2 138.2 %all-gather.4.cloned.1.call-start = ((), (), s32[]{:S(2)}) async-start(), calls=%async_computation | async-start | bytes 2162688 | tf_op jit(solution)/shard_map/all_gather | solution.py:754
  8.9 312.5 %all-gather.6.cloned.1.call-start = ((), (), s32[]{:S(2)}) async-start(), calls=%async_computation.1 | async-start | bytes 3604480 | tf_op jit(solution)/shard_map/all_gather | solution.py:297
  11.3 106.9 %collective-permute-start.6 = (bf16[352,1024]{1,0:T(8,128)(2,1)}, bf16[352,1024]{1,0:T(8,128)(2,1)}, u32[]{:S(2)}, u32[]{:S(2)}) collective-permute-start(bf16[352,1024]{1,0:T(8,128)(2,1)} %convert_bitcast_fusion.3), channel_id=1, source_target_pairs={{1,4},{3,6},{4,1},{6,3},{9,12},{11,14},{12,9},{14,11},{17,20},{19,... | collective-permute-start | bytes 2162696 | tf_op jit(solution)/shard_map/ppermute | solution.py:54
  16.1 65.7 %collective-permute-start.1 = (bf16[128,2816]{1,0:T(8,128)(2,1)}, bf16[128,2816]{1,0:T(8,128)(2,1)}, u32[]{:S(2)}, u32[]{:S(2)}) collective-permute-start(bf16[128,2816]{1,0:T(8,128)(2,1)} %convert_bitcast_fusion.4), channel_id=1, source_target_pairs={{1,4},{3,6},{4,1},{6,3},{9,12},{11,14},{12,9},{14,11},{17,20},{19,... | collective-permute-start | bytes 2162696 | tf_op jit(solution)/shard_map/ppermute | solution.py:54
  19.1 65.3 %collective-permute-start = (bf16[128,2816]{1,0:T(8,128)(2,1)}, bf16[128,2816]{1,0:T(8,128)(2,1)}, u32[]{:S(2)}, u32[]{:S(2)}) collective-permute-start(bf16[128,2816]{1,0:T(8,128)(2,1)} %convert_bitcast_fusion.5), channel_id=1, source_target_pairs={{1,4},{3,6},{4,1},{6,3},{9,12},{11,14},{12,9},{14,11},{17,20},{19,... | collective-permute-start | bytes 2162696 | tf_op jit(solution)/shard_map/ppermute | solution.py:54
  118.2 138.4 %collective-permute-start.11 = (bf16[128,2816]{1,0:T(8,128)(2,1)}, bf16[128,2816]{1,0:T(8,128)(2,1)}, u32[]{:S(2)}, u32[]{:S(2)}) collective-permute-start(bf16[128,2816]{1,0:T(8,128)(2,1)} %broadcast_select_fusion.11.refs_0_), channel_id=1, source_target_pairs={{0,1},{1,0},{2,3},{3,2},{4,5},{5,4},{6,7},{7,6},{8,9},{9,8},{10,11... | collective-permute-start | bytes 2162696 | tf_op jit(solution)/shard_map/ppermute | solution.py:36
  143.6 50.9 %collective-permute-start.10 = (bf16[128,2816]{1,0:T(8,128)(2,1)}, bf16[128,2816]{1,0:T(8,128)(2,1)}, u32[]{:S(2)}, u32[]{:S(2)}) collective-permute-start(bf16[128,2816]{1,0:T(8,128)(2,1)} %collective-permute-done.5), channel_id=1, source_target_pairs={{8,0},{9,1},{10,2},{11,3},{12,4},{13,5},{14,6},{15,7},{16,8},{17,9... | collective-permute-start | bytes 2162696 | tf_op jit(solution)/shard_map/ppermute | solution.py:281
  149.5 107.2 %collective-permute-start.17 = (bf16[128,2816]{1,0:T(8,128)(2,1)S(1)}, bf16[128,2816]{1,0:T(8,128)(2,1)S(1)}, u32[]{:S(2)}, u32[]{:S(2)}) collective-permute-start(bf16[128,2816]{1,0:T(8,128)(2,1)S(1)} %copy-done.80), channel_id=1, source_target_pairs={{0,1},{1,0},{2,3},{3,2},{4,5},{5,4},{6,7},{7,6},{8,9},{9,8},{10,11... | collective-permute-start | bytes 2162696 | tf_op jit(solution)/shard_map/ppermute | solution.py:36
  195.2 43.7 %collective-permute-start.15 = (bf16[128,2816]{1,0:T(8,128)(2,1)}, bf16[128,2816]{1,0:T(8,128)(2,1)S(1)}, u32[]{:S(2)}, u32[]{:S(2)}) collective-permute-start(bf16[128,2816]{1,0:T(8,128)(2,1)} %collective-permute-done.8), channel_id=1, source_target_pairs={{8,0},{9,1},{10,2},{11,3},{12,4},{13,5},{14,6},{15,7}} | collective-permute-start | bytes 2162696 | tf_op jit(solution)/shard_map/ppermute | solution.py:281
  199.7 54.7 %collective-permute-start.21 = (bf16[128,2816]{1,0:T(8,128)(2,1)}, bf16[128,2816]{1,0:T(8,128)(2,1)S(1)}, u32[]{:S(2)}, u32[]{:S(2)}) collective-permute-start(bf16[128,2816]{1,0:T(8,128)(2,1)} %collective-permute-done.10), channel_id=1, source_target_pairs={{8,0},{9,1},{10,2},{11,3},{12,4},{13,5},{14,6},{15,7}} | collective-permute-start | bytes 2162696 | tf_op jit(solution)/shard_map/ppermute | solution.py:281
  202.3 55.0 %collective-permute-start.20 = (bf16[128,2816]{1,0:T(8,128)(2,1)S(1)}, bf16[128,2816]{1,0:T(8,128)(2,1)S(1)}, u32[]{:S(2)}, u32[]{:S(2)}) collective-permute-start(bf16[128,2816]{1,0:T(8,128)(2,1)S(1)} %broadcast_select_fusion.2.refs_12_), channel_id=1, source_target_pairs={{0,1},{1,0},{2,3},{3,2},{4,5},{5,4},{6,7},{7,6},{8,9},{9,8},{10,11... | collective-permute-start | bytes 2162696 | tf_op jit(solution)/shard_map/ppermute | solution.py:36
  239.0 53.2 %collective-permute-start.14 = (bf16[128,2816]{1,0:T(8,128)(2,1)S(1)}, bf16[128,2816]{1,0:T(8,128)(2,1)S(1)}, u32[]{:S(2)}, u32[]{:S(2)}) collective-permute-start(bf16[128,2816]{1,0:T(8,128)(2,1)S(1)} %broadcast_select_fusion.3.refs_4_), channel_id=1, source_target_pairs={{0,1},{1,0},{2,3},{3,2},{4,5},{5,4},{6,7},{7,6},{8,9},{9,8},{10,11... | collective-permute-start | bytes 2162696 | tf_op jit(solution)/shard_map/ppermute | solution.py:36
  254.4 37.8 %collective-permute-start.13 = (bf16[128,2816]{1,0:T(8,128)(2,1)S(1)}, bf16[128,2816]{1,0:T(8,128)(2,1)S(1)}, u32[]{:S(2)}, u32[]{:S(2)}) collective-permute-start(bf16[128,2816]{1,0:T(8,128)(2,1)S(1)} %broadcast_select_fusion.5.refs_2_), channel_id=1, source_target_pairs={{0,1},{1,0},{2,3},{3,2},{4,5},{5,4},{6,7},{7,6},{8,9},{9,8},{10,11... | collective-permute-start | bytes 2162696 | tf_op jit(solution)/shard_map/ppermute | solution.py:36
  256.6 35.6 %collective-permute-start.16 = (bf16[128,2816]{1,0:T(8,128)(2,1)S(1)}, bf16[128,2816]{1,0:T(8,128)(2,1)S(1)}, u32[]{:S(2)}, u32[]{:S(2)}) collective-permute-start(bf16[128,2816]{1,0:T(8,128)(2,1)S(1)} %broadcast_select_fusion.1.refs_6_), channel_id=1, source_target_pairs={{0,1},{1,0},{2,3},{3,2},{4,5},{5,4},{6,7},{7,6},{8,9},{9,8},{10,11... | collective-permute-start | bytes 2162696 | tf_op jit(solution)/shard_map/ppermute | solution.py:36
  256.7 35.5 %collective-permute-start.19 = (bf16[128,2816]{1,0:T(8,128)(2,1)S(1)}, bf16[128,2816]{1,0:T(8,128)(2,1)S(1)}, u32[]{:S(2)}, u32[]{:S(2)}) collective-permute-start(bf16[128,2816]{1,0:T(8,128)(2,1)S(1)} %broadcast_select_fusion.4.refs_10_), channel_id=1, source_target_pairs={{0,1},{1,0},{2,3},{3,2},{4,5},{5,4},{6,7},{7,6},{8,9},{9,8},{10,11... | collective-permute-start | bytes 2162696 | tf_op jit(solution)/shard_map/ppermute | solution.py:36
  364.7 87.2 %collective-permute-start.32 = (bf16[4,128,2816]{2,1,0:T(8,128)(2,1)}, bf16[4,128,2816]{2,1,0:T(8,128)(2,1)}, u32[]{:S(2)}, u32[]{:S(2)}) collective-permute-start(bf16[4,128,2816]{2,1,0:T(8,128)(2,1)} %dynamic-slice_bitcast_fusion), channel_id=1, source_target_pairs={{0,1},{1,0},{2,3},{3,2},{4,5},{5,4},{6,7},{7,6},{8,9},{9,8},{10,11... | collective-permute-start | bytes 8650760 | tf_op jit(solution)/shard_map/ppermute | solution.py:36
  378.0 83.9 %collective-permute-start.29 = (bf16[4,128,2816]{2,1,0:T(8,128)(2,1)}, bf16[4,128,2816]{2,1,0:T(8,128)(2,1)}, u32[]{:S(2)}, u32[]{:S(2)}) collective-permute-start(bf16[4,128,2816]{2,1,0:T(8,128)(2,1)} %dynamic-slice_bitcast_fusion.1), channel_id=1, source_target_pairs={{0,1},{1,0},{2,3},{3,2},{4,5},{5,4},{6,7},{7,6},{8,9},{9,8},{10,11... | collective-permute-start | bytes 8650760 | tf_op jit(solution)/shard_map/ppermute | solution.py:36
  386.6 61.1 %collective-permute-start.49 = (bf16[352,1024]{1,0:T(8,128)(2,1)}, bf16[352,1024]{1,0:T(8,128)(2,1)}, u32[]{:S(2)}, u32[]{:S(2)}) collective-permute-start(bf16[352,1024]{1,0:T(8,128)(2,1)} %get-tuple-element.433), channel_id=1, source_target_pairs={{0,8},{1,9},{2,10},{3,11},{4,12},{5,13},{6,14},{7,15},{8,16},{9,17... | collective-permute-start | bytes 2162696 | tf_op jit(solution)/shard_map/ppermute | solution.py:361
  391.6 56.1 %collective-permute-start.50 = (bf16[352,1024]{1,0:T(8,128)(2,1)S(1)}, bf16[352,1024]{1,0:T(8,128)(2,1)}, u32[]{:S(2)}, u32[]{:S(2)}) collective-permute-start(bf16[352,1024]{1,0:T(8,128)(2,1)S(1)} %get-tuple-element.434), channel_id=1, source_target_pairs={{8,0},{9,1},{10,2},{11,3},{12,4},{13,5},{14,6},{15,7},{16,8},{17,9... | collective-permute-start | bytes 2162696 | tf_op jit(solution)/shard_map/ppermute | solution.py:361
  522.2 87.3 %collective-permute-start.45 = (bf16[2,8,32,1024]{3,2,1,0:T(8,128)(2,1)}, bf16[2,8,32,1024]{3,2,1,0:T(8,128)(2,1)}, u32[]{:S(2)}, u32[]{:S(2)}) collective-permute-start(bf16[2,8,32,1024]{3,2,1,0:T(8,128)(2,1)} %bitcast.327), channel_id=1, source_target_pairs={{0,1},{1,0},{2,3},{3,2},{4,5},{5,4},{6,7},{7,6},{8,9},{9,8},{10,11... | collective-permute-start | bytes 3145736 | tf_op jit(solution)/shard_map/ppermute | solution.py:36
  609.5 72.0 %collective-permute-start.43 = (bf16[2,8,3,32,256]{4,3,2,1,0:T(8,128)(2,1)S(1)}, bf16[2,8,3,32,256]{4,3,2,1,0:T(8,128)(2,1)S(1)}, u32[]{:S(2)}, u32[]{:S(2)}) collective-permute-start(bf16[2,8,3,32,256]{4,3,2,1,0:T(8,128)(2,1)S(1)} %bitcast.383), channel_id=1, source_target_pairs={{0,1},{1,0},{2,3},{3,2},{4,5},{5,4},{6,7},{7,6},{8,9},{9,8},{10,11... | collective-permute-start | bytes 2359304 | tf_op jit(solution)/shard_map/ppermute | solution.py:36
  613.8 71.2 %collective-permute-start.46 = (bf16[8,32,1024]{2,1,0:T(8,128)(2,1)}, bf16[8,32,1024]{2,1,0:T(8,128)(2,1)}, u32[]{:S(2)}, u32[]{:S(2)}) collective-permute-start(bf16[8,32,1024]{2,1,0:T(8,128)(2,1)} %dynamic-slice_bitcast_fusion.9), channel_id=1, source_target_pairs={{0,2},{1,3},{2,0},{3,1},{4,6},{5,7},{6,4},{7,5},{8,10},{9,11},{10,... | collective-permute-start | bytes 1572872 | tf_op jit(solution)/shard_map/ppermute | solution.py:36
  670.4 72.0 %collective-permute-start.47 = (bf16[128,2816]{1,0:T(8,128)(2,1)}, bf16[128,2816]{1,0:T(8,128)(2,1)}, u32[]{:S(2)}, u32[]{:S(2)}) collective-permute-start(bf16[128,2816]{1,0:T(8,128)(2,1)} %fusion.35), channel_id=1, source_target_pairs={{1,4},{3,6},{4,1},{6,3},{9,12},{11,14},{12,9},{14,11},{17,20},{19,... | collective-permute-start | bytes 2162696 | tf_op jit(solution)/shard_map/ppermute | solution.py:54
  678.7 58.7 %collective-permute-start.48 = (bf16[128,2816]{1,0:T(8,128)(2,1)}, bf16[128,2816]{1,0:T(8,128)(2,1)S(1)}, u32[]{:S(2)}, u32[]{:S(2)}) collective-permute-start(bf16[128,2816]{1,0:T(8,128)(2,1)} %fusion.33), channel_id=1, source_target_pairs={{1,4},{3,6},{4,1},{6,3},{9,12},{11,14},{12,9},{14,11},{17,20},{19,... | collective-permute-start | bytes 2162696 | tf_op jit(solution)/shard_map/ppermute | solution.py:54
  (153 other events, 2247.3 us)
Sparse Core Ops, SparseCore 0:
  11.5 71.4 all-gather.3
  145.5 81.9 all-gather.5
where the time goes:
time: 769 us; the launch traced here: 755 us
  Pallas kernels  302 us (39%)
  waiting for transfers between devices  154 us (20%)
  starting transfers between devices  107 us (14%)
  other arithmetic  79.9 us (10%)
  local copies, waits for them, and re-layouts  49.9 us (6%)
  matrix products  45.4 us (6%)
  between operations  16.6 us (2%)
    pallas_call x7, Pallas kernels, exchange_call(): pl.pallas_call(kernel, in_specs=[vmem] * len(arrays), out_specs=[vmem] *...  225 us
    ppermute x12, waiting for transfers between devices, line_permute(): return lax.ppermute(value, both, pairs)  86.6 us
    ppermute x18, waiting for transfers between devices, scatter_permute(): return lax.ppermute(value, both, pairs)  57.6 us
    ppermute x18, starting transfers between devices, scatter_permute(): return lax.ppermute(value, both, pairs)  45 us
    pallas_call x1, Pallas kernels, attend_back(): pl.pallas_call(partial(attend_back_kernel, blocks, heads), grid=(steps,),...  25.3 us
    unnamed x254, local copies, waits for them, and re-layouts  24.5 us
    ppermute x12, starting transfers between devices, line_permute(): return lax.ppermute(value, both, pairs)  22.4 us
    ppermute x6, starting transfers between devices, turn(): lax.ppermute(value, both, [(d, other(d)) for d in range(count) if other(d...  20.8 us
  transfers between devices with their start and end apart: 54, of which 16 were waited for; matrix products, arithmetic and copies ran while one was open for 18% of the time, Pallas kernels for 40%

commit v1 on v0

--- a/solution.py
+++ b/solution.py
@@ -183,41 +183,47 @@
     )[0]
 
 
-def closing_kernel(cycle, col_ref, out_in, small_ref, col_out, out_out, all_ref, s1, r1, s2, r2, s3, r3):
+def closing_kernel(
+    cycle, col_ref, out_in, small_ref, col_out, out_out, mid_ref, all_ref, s1, r1, s2, r2, s3, r3, s4, r4
+):
     me = flat_index()
-    ctx, _ = place_of(me)
-    count = cycle * EXP_AXIS
-    greet([me ^ rel for rel in range(1, count)])
-    copies = []
-    for source, target, send, recv in ((col_ref, col_out, s1, r1), (out_in, out_out, s2, r2)):
+    ctx, exp = place_of(me)
+    greet([me ^ (rel * EXP_AXIS) for rel in range(1, cycle)] + [me ^ rel for rel in range(1, EXP_AXIS)])
+    smalls, copies = [], []
+    for source, target, send, recv, out in (
+        (small_ref, mid_ref, s3, r3, smalls), (col_ref, col_out, s1, r1, copies),
+        (out_in, out_out, s2, r2, copies),
+    ):
         for rel in range(1, cycle):
-            copies.append(
+            out.append(
                 remote(
                     source.at[ctx ^ rel], target.at[ctx], send.at[rel], recv.at[rel],
                     me ^ (rel * EXP_AXIS),
                 )
             )
-    for rel in range(1, count):
-        copies.append(
-            remote(small_ref.at[me ^ rel], all_ref.at[me], s3.at[rel], r3.at[rel], me ^ rel)
-        )
-    for copy in copies:
-        copy.start()
+            out[-1].start()
+    mid_ref[ctx] = small_ref[ctx]
     col_out[ctx] = col_ref[ctx]
     out_out[ctx] = out_in[ctx]
-    all_ref[me] = small_ref[me]
+    for copy in smalls:
+        copy.wait()
+    for rel in range(1, EXP_AXIS):
+        copies.append(remote(mid_ref, all_ref.at[exp], s4.at[rel], r4.at[rel], me ^ rel))
+        copies[-1].start()
+    all_ref[exp] = mid_ref[...]
     for copy in copies:
         copy.wait()
 
 
 def closing(cols, out, small):
     cycle = lax.axis_size("ctx")
-    count = cycle * EXP_AXIS
-    return exchange_call(
+    results = exchange_call(
         partial(closing_kernel, cycle), 6, [cols, out, small],
-        [jax.ShapeDtypeStruct(x.shape, x.dtype) for x in (cols, out, small)],
-        [cycle, cycle, cycle, cycle, count, count],
-    )
+        [jax.ShapeDtypeStruct(x.shape, x.dtype) for x in (cols, out, small)]
+        + [jax.ShapeDtypeStruct((EXP_AXIS,) + small.shape, small.dtype)],
+        [cycle] * 6 + [EXP_AXIS] * 2,
+    )
+    return results[0], results[1], results[3]
 
 
 def plane_kernel(forward, arrays, *refs):
@@ -310,55 +316,9 @@
     return (mine.astype(f32) + got.astype(f32)).astype(bf16)
 
 
-class LineScatter:
-    def __init__(self, halves):
-        self.halves = halves
-        self.size = halves[0].shape[0]
-        self.place = lax.axis_index("ctx") // 2
-        self.got = [[None, None] for _ in halves]
-
-    def part(self, index, place, got):
-        own = lax.dynamic_index_in_dim(
-            self.halves[index], jnp.clip(place, 0, self.size - 1), 0, keepdims=False
-        )
-        return own if got is None else (own.astype(f32) + got.astype(f32)).astype(bf16)
-
-    def round(self, step):
-        away = self.size - 1 - step
-        for index in range(len(self.halves)):
-            pair = self.got[index]
-            values = (
-                self.part(index, self.place + away, pair[0]),
-                self.part(index, self.place - away, pair[1]),
-            )
-            pair[0] = scatter_permute(values[0], 1, step)
-            pair[1] = scatter_permute(values[1], -1, step)
-
-    def settle(self, values):
-        flat = [x for pair in self.got for x in pair]
-        out = lax.optimization_barrier((*values, *flat))
-        flat = out[len(values) :]
-        self.got = [[flat[2 * k], flat[2 * k + 1]] for k in range(len(self.got))]
-        return out[: len(values)]
-
-    def totals(self):
-        out = []
-        for index, (right, left) in enumerate(self.got):
-            own = lax.dynamic_index_in_dim(self.halves[index], self.place, 0, keepdims=False)
-            total = own.astype(f32) + right.astype(f32) + left.astype(f32)
-            out.append(turn(total.astype(bf16)))
-        return out
-
-
-def scatter_permute(value, step, number):
-    size = lax.axis_size("ctx") // 2
-    pairs = []
-    for a in range(size):
-        b = a + step
-        if 0 <= b < size and (a <= number if step > 0 else a >= size - 1 - number):
-            for low in range(2 * EXP_AXIS):
-                pairs.append((a * 2 * EXP_AXIS + low, b * 2 * EXP_AXIS + low))
-    return lax.ppermute(value, both, pairs)
+def scatter_expert(half):
+    part = lax.psum_scatter(half, "ctx", scatter_dimension=0, axis_index_groups=pair_groups())
+    return turn(part)
 
 
 def gelu_pair(value):
@@ -383,9 +343,9 @@
 
 
 def expert_front_kernel(count, rows_ref, *refs):
-    gates, ups = refs[:count], refs[count : 2 * count]
-    units_ref, value_ref, slope_ref, turned = refs[2 * count :]
-    block = gates[0].shape[0]
+    blocks = refs[:count]
+    units_ref, value_ref, slope_ref, turned = refs[count:]
+    block = blocks[0].shape[1]
 
     @pl.when(pl.program_id(0) == 0)
     def _():
@@ -393,22 +353,22 @@
             turned[:, k * block : (k + 1) * block] = rows_ref[:, places]
 
     rows = turned[...]
-    gate = jnp.dot(rows, jnp.concatenate([r[...] for r in gates], 0), preferred_element_type=f32)
-    up = jnp.dot(rows, jnp.concatenate([r[...] for r in ups], 0), preferred_element_type=f32)
+    gate = jnp.dot(rows, jnp.concatenate([r[0] for r in blocks], 0), preferred_element_type=f32)
+    up = jnp.dot(rows, jnp.concatenate([r[1] for r in blocks], 0), preferred_element_type=f32)
     value, slope = gelu_pair(gate)
     units_ref[...] = (value * up).astype(bf16)
     value_ref[...] = value.astype(bf16)
     slope_ref[...] = (slope * up).astype(bf16)
 
 
-def expert_front(rows, gates, ups):
-    count, cols, tile = len(gates), gates[0].shape[1], 256
+def expert_front(rows, blocks):
+    count, cols, tile = len(blocks), blocks[0].shape[2], 256
     wide = pl.BlockSpec((rows.shape[0], tile), lambda j: (0, j))
     return pl.pallas_call(
         partial(expert_front_kernel, count),
         grid=(cols // tile,),
         in_specs=[pl.BlockSpec(rows.shape, lambda j: (0, 0))]
-        + [pl.BlockSpec((gates[0].shape[0], tile), lambda j: (0, j))] * (2 * count),
+        + [pl.BlockSpec(blocks[0].shape[:2] + (tile,), lambda j: (0, 0, j))] * count,
         out_specs=[wide] * 3,
         out_shape=[jax.ShapeDtypeStruct((rows.shape[0], cols), bf16)] * 3,
         scratch_shapes=[pltpu.VMEM(rows.shape, bf16)],
@@ -417,7 +377,7 @@
             flops=4 * rows.size * cols, bytes_accessed=4 * D * cols, transcendentals=0
         ),
         name="expert_front",
-    )(rows, *gates, *ups)
+    )(rows, *blocks)
 
 
 def expert_middle_kernel(grads_ref, down_ref, value_ref, slope_ref, gate_ref, up_ref):
@@ -449,11 +409,11 @@
 
 
 def expert_rear_kernel(count, gate_ref, up_ref, *refs):
-    gates, ups = refs[:count], refs[count : 2 * count]
-    out_ref, total = refs[2 * count :]
-    block = gates[0].shape[0]
+    blocks = refs[:count]
+    out_ref, total = refs[count:]
+    block = blocks[0].shape[1]
     weights = jnp.concatenate(
-        [jnp.concatenate([r[...] for r in gates], 0), jnp.concatenate([r[...] for r in ups], 0)], 1
+        [jnp.concatenate([r[part] for r in blocks], 0) for part in range(2)], 1
     )
     grads = jnp.concatenate([gate_ref[...], up_ref[...]], 1)
     term = lax.dot_general(grads, weights, last_dims, preferred_element_type=f32)
@@ -472,15 +432,15 @@
             out_ref[:, places] = total[:, k * block : (k + 1) * block].astype(bf16)
 
 
-def expert_rear(grad_gate, grad_up, gates, ups):
-    count, cols, tile = len(gates), gates[0].shape[1], 256
+def expert_rear(grad_gate, grad_up, blocks):
+    count, cols, tile = len(blocks), blocks[0].shape[2], 256
     wide = pl.BlockSpec((grad_gate.shape[0], tile), lambda j: (0, j))
     shape = (grad_gate.shape[0], D)
     return pl.pallas_call(
         partial(expert_rear_kernel, count),
         grid=(cols // tile,),
         in_specs=[wide] * 2
-        + [pl.BlockSpec((gates[0].shape[0], tile), lambda j: (0, j))] * (2 * count),
+        + [pl.BlockSpec(blocks[0].shape[:2] + (tile,), lambda j: (0, 0, j))] * count,
         out_specs=pl.BlockSpec(shape, lambda j: (0, 0)),
         out_shape=jax.ShapeDtypeStruct(shape, bf16),
         scratch_shapes=[pltpu.VMEM(shape, f32)],
@@ -489,7 +449,7 @@
             flops=4 * shape[0] * D * cols, bytes_accessed=4 * D * cols, transcendentals=0
         ),
         name="expert_rear",
-    )(grad_gate, grad_up, *gates, *ups)
+    )(grad_gate, grad_up, *blocks)
 
 
 def lane_mask(width, head, dtype):
@@ -752,26 +712,19 @@
     small = jnp.pad(small, (0, 16 * width - small_size)).reshape(1, 16, width)
     cols = jnp.concatenate([cols, jnp.broadcast_to(small, (group, 16, width))], axis=1)
     w_out = lax.all_gather(out_master.astype(bf16), both, axis=0, tiled=True)
-    gate_own, up_own, down_own = (
-        turn(member[0].astype(bf16)) for member in (gate_master, up_master, down_master)
-    )
+    pair_own = turn(jnp.concatenate([gate_master, up_master], axis=0).astype(bf16))
+    down_own = turn(down_master[0].astype(bf16))
     seq, gathered = opening(tok, cols)
-    gate_own, up_own, seq, gathered = lax.optimization_barrier((gate_own, up_own, seq, gathered))
-    lines = [[own, own] for own in (gate_own, up_own)]
-    right, left = [], []
+    pair_own, seq, gathered = lax.optimization_barrier((pair_own, seq, gathered))
+    right, left = [pair_own], [pair_own]
 
     def line_round(step):
-        for pair in lines:
-            pair[0] = line_permute(pair[0], 1, step)
-            pair[1] = line_permute(pair[1], -1, step)
-        right.append([pair[0] for pair in lines])
-        left.append([pair[1] for pair in lines])
+        right.append(line_permute(right[-1], 1, step))
+        left.append(line_permute(left[-1], -1, step))
 
     def line_settle(value):
-        flat = lax.optimization_barrier((value, *[x for pair in lines for x in pair]))
-        lines[0][0], lines[0][1], lines[1][0], lines[1][1] = flat[1:]
-        right[-1], left[-1] = [flat[1], flat[3]], [flat[2], flat[4]]
-        return flat[0]
+        value, right[-1], left[-1] = lax.optimization_barrier((value, right[-1], left[-1]))
+        return value
 
     line_round(0)
     seq = seq.reshape(length, D)
@@ -802,7 +755,7 @@
 
     attended = line_settle(attended)
     back = cycle_swap(attended.reshape(cycle, tok_rows, width), 1)
-    back, down_own = lax.optimization_barrier((line_settle(back), down_own))
+    back = line_settle(back)
     line_round(1)
     toks = micro * tok_rows
     attended_bf = back.reshape(micro, group, tok_rows, width).transpose(0, 2, 1, 3)
@@ -840,7 +793,7 @@
         jnp.concatenate(hits, axis=0), jnp.concatenate(scaled_dy, axis=0), first_dims,
         preferred_element_type=f32,
     )
-    sent_rows = line_settle(sent_rows.astype(bf16))
+    sent_rows, down_own = lax.optimization_barrier((line_settle(sent_rows.astype(bf16)), down_own))
     if line > 3:
         line_round(2)
     got_rows, got_grads = plane_swap(
@@ -851,52 +804,44 @@
     flat_rows = got_rows.reshape(-1, D)
     flat_grads = got_grads.reshape(-1, D)
 
-    def blocks_of(index, own):
-        blocks = [own] + [
-            jnp.where(line_place + k < line, left[k - 1][index], right[line - 1 - k][index])
-            for k in range(1, line)
-        ]
-        return [block for mine in blocks for block in (mine, swap_bit(mine, 0))]
-
-    gates, ups = blocks_of(0, gate_own), blocks_of(1, up_own)
+    blocks = []
+    for k in range(line):
+        mine = pair_own
+        if k:
+            mine = jnp.where(line_place + k < line, left[k], right[line - k])
+        blocks += [mine, swap_bit(mine, 0)]
     w_down = gather_expert(down_own)
-    kernels = gate_own.shape[0] % 128 == 0
+    kernels = pair_own.shape[1] % 128 == 0
     if kernels:
-        units, value, slope = expert_front(flat_rows, gates, ups)
+        units, value, slope = expert_front(flat_rows, blocks)
     else:
 
-        def whole(blocks):
+        def whole(part):
             pieces = []
             for mine, theirs in zip(blocks[::2], blocks[1::2]):
-                pieces += [jnp.where(low, mine, theirs), jnp.where(low, theirs, mine)]
+                pieces += [jnp.where(low, mine, theirs)[part], jnp.where(low, theirs, mine)[part]]
             return jnp.concatenate(pieces, axis=0)
 
         def turned(value, shift):
             twice = jnp.concatenate([value, value], axis=1)
             return lax.dynamic_slice_in_dim(twice, shift * (D // line), D, 1)
 
-        w_gate, w_up = whole(gates), whole(ups)
+        w_gate, w_up = whole(0), whole(1)
         turned_rows = turned(flat_rows, line_place)
         gate_pre = jnp.dot(turned_rows, w_gate, preferred_element_type=f32)
         up_pre = jnp.dot(turned_rows, w_up, preferred_element_type=f32)
         value, slope = gelu_pair(gate_pre)
         units, slope = (value * up_pre).astype(bf16), slope * up_pre
     down_grad = lax.dot_general(units, flat_grads, first_dims, preferred_element_type=f32)
-    down_line = LineScatter([core_sum(down_grad.astype(bf16))])
-    down_line.round(0)
+    down_sum = scatter_expert(core_sum(down_grad.astype(bf16)))
     grad_gate, grad_up = expert_middle(flat_grads, w_down, value, slope)
-    (grad_up,) = down_line.settle((grad_up,))
-    down_line.round(1)
     up_grad = lax.dot_general(flat_rows, grad_up, first_dims, preferred_element_type=f32)
+    up_sum = scatter_expert(core_sum(up_grad.astype(bf16)))
     gate_grad = lax.dot_general(flat_rows, grad_gate, first_dims, preferred_element_type=f32)
-    both_line = LineScatter([core_sum(up_grad.astype(bf16)), core_sum(gate_grad.astype(bf16))])
-    (grad_gate,) = down_line.settle((grad_gate,))
-    for step in range(2, line - 1):
-        down_line.round(step)
-    both_line.round(0)
+    gate_sum = scatter_expert(core_sum(gate_grad.astype(bf16)))
     out_rows = jnp.dot(units, w_down, preferred_element_type=f32).astype(bf16)
     if kernels:
-        grad_rows = expert_rear(grad_gate, grad_up, gates, ups)
+        grad_rows = expert_rear(grad_gate, grad_up, blocks)
     else:
         grad_rows = lax.dot_general(grad_gate, w_gate, last_dims, preferred_element_type=f32)
         grad_rows = grad_rows + lax.dot_general(
@@ -904,8 +849,6 @@
         )
         grad_rows = turned(grad_rows.astype(bf16), line - line_place)
     back_out, back_grad = plane_swap((out_rows.reshape(slots), grad_rows.reshape(slots)), False, 3)
-    back_out, back_grad = both_line.settle((back_out, back_grad))
-    both_line.round(1)
     back_out, back_grad = back_out.reshape(slot_count, D), back_grad.reshape(slot_count, D)
 
     returned = [jnp.dot(hit, back_out, preferred_element_type=f32) for hit in hits]
@@ -931,10 +874,7 @@
     grad_attended = lax.dot_general(grad_branch, w_out, last_dims, preferred_element_type=f32)
     grad_attended = grad_attended.astype(bf16).reshape(micro, tok_rows, group, width)
     grad_attended = grad_attended.transpose(0, 2, 1, 3).reshape(cycle, tok_rows, width)
-    (grad_attended,) = both_line.settle((grad_attended,))
     grad_attended = cycle_swap(grad_attended, 4).reshape(length, width)
-    for step in range(2, line - 1):
-        both_line.round(step)
     out_grad = lax.dot_general(attended_bf, grad_branch, first_dims, preferred_element_type=f32)
     out_grad = out_grad.astype(bf16).reshape(cycle, 2, 2, rows, D).transpose(2, 1, 0, 3, 4)
     out_grad = cube_sum(out_grad, 0)
@@ -947,8 +887,7 @@
     qkv_grad = cube_sum(qkv_grad, 0)
     qkv_grad = cube_sum(qkv_grad, 1)
     partial_normed = jnp.einsum("cte,cde->td", dqkv, w_qkv, preferred_element_type=f32)
-    (partial_normed,) = both_line.settle((partial_normed.astype(bf16),))
-    partial_normed = partial_normed.reshape(cycle, tok_rows, D)
+    partial_normed = partial_normed.astype(bf16).reshape(cycle, tok_rows, D)
     pieces = cycle_swap(partial_normed, 5)
     grad_normed_attn = jnp.sum(pieces.reshape(micro, group, tok_rows, D).astype(f32), axis=1)
     grad_inputs, gain_attn_grad = norm_back(
@@ -956,8 +895,6 @@
     )
     grad_inputs = grad_inputs + grad_hidden
 
-    (down_sum,) = down_line.totals()
-    up_sum, gate_sum = both_line.totals()
     blocks = length // BLOCK
     offset_grad = jnp.zeros((own_heads, 2 * length), f32)
     for d in range(blocks):
@@ -978,11 +915,14 @@
         axis=1,
     )
     small_grads = jnp.pad(small_grads, ((0, 0), (0, -small_grads.shape[1] % 128)))
-    qkv_grad, out_grad, small_parts = closing(qkv_grad, out_grad, small_grads[:, None])
+    small_grads = small_grads.reshape(cycle, EXP_AXIS, 1, -1)
+    qkv_grad, out_grad, small_parts = closing(qkv_grad, out_grad, small_grads)
     qkv_sum = jnp.sum(qkv_grad.reshape(micro, group, 3, rows, width).astype(f32), axis=0)
     qkv_sum = qkv_sum.transpose(1, 2, 0, 3).reshape(3, rows, D)
     out_sum = jnp.sum(out_grad.astype(f32), axis=0)
-    small_sum = jnp.sum(small_parts[:, 0], axis=0)[:small_size]
+    small_sum = jnp.sum(small_parts, axis=(0, 1))
+    small_sum = lax.dynamic_index_in_dim(small_sum, lax.axis_index("exp"), 0, keepdims=False)
+    small_sum = small_sum[0, :small_size]
     gradients = (
         qkv_sum,
         out_sum,

time: 769 us -> 717 us (0.932)
  starting transfers between devices: 107 us -> 46.7 us
  Pallas kernels: 302 us -> 344 us
  local copies, waits for them, and re-layouts: 49.9 us -> 34.4 us
  other arithmetic: 79.9 us -> 67.3 us
    ppermute x18 -> x0, waiting for transfers between devices: 57.6 us -> none  [scatter_permute(): return lax.ppermute(value, both, pairs)]
    ppermute x18 -> x0, starting transfers between devices: 45 us -> none  [scatter_permute(): return lax.ppermute(value, both, pairs)]
    pallas_call x7, Pallas kernels: 225 us -> 268 us  [exchange_call(): pl.pallas_call(kernel, in_specs=[vmem] * len(arrays), out_specs=[vmem] *...]
    ppermute x12 -> x6, waiting for transfers between devices: 86.6 us -> 123 us  [line_permute(): return lax.ppermute(value, both, pairs)]
    convert_element_type x12 -> x1, other arithmetic: 18.5 us -> 0.97 us  [layer(): down_own = turn(down_master[0].astype(bf16))]
    ppermute x16 -> x12, starting transfers between devices: 19 us -> 6.87 us  [swap_bit(): return lax.ppermute(value, both, [(d, d ^ 1 << bit) for d in range(count)])]
    ppermute x16 -> x12, waiting for transfers between devices: 9.74 us -> 21.4 us  [swap_bit(): return lax.ppermute(value, both, [(d, d ^ 1 << bit) for d in range(count)])]
    unnamed x254 -> x216, local copies, waits for them, and re-layouts: 24.5 us -> 17.5 us
  transfers between devices with their start and end apart: 54 -> 28, of which waited for: 16 -> 9; matrix products, arithmetic and copies ran while one was open for 18% -> 18% of each run, Pallas kernels for 40% -> 49%
where the time goes in v1:
time: 717 us; the launch traced here: 705 us
  Pallas kernels  344 us (48%)
  waiting for transfers between devices  152 us (21%)
  other arithmetic  67.3 us (9%)
  starting transfers between devices  46.7 us (7%)
  matrix products  44.8 us (6%)
  local copies, waits for them, and re-layouts  34.4 us (5%)
  between operations  16.2 us (2%)
    pallas_call x7, Pallas kernels, exchange_call(): pl.pallas_call(kernel, in_specs=[vmem] * len(arrays), out_specs=[vmem] *...  268 us
    ppermute x6, waiting for transfers between devices, line_permute(): return lax.ppermute(value, both, pairs)  123 us
    pallas_call x1, Pallas kernels, attend_back(): pl.pallas_call(partial(attend_back_kernel, blocks, heads), grid=(steps,),...  25.1 us
    ppermute x12, waiting for transfers between devices, swap_bit(): return lax.ppermute(value, both, [(d, d ^ 1 << bit) for d in range(count)])  21.4 us
    ppermute x6, starting transfers between devices, line_permute(): return lax.ppermute(value, both, pairs)  19.9 us
    ppermute x5, starting transfers between devices, turn(): lax.ppermute(value, both, [(d, other(d)) for d in range(count) if other(d...  19.4 us
    pallas_call x1, Pallas kernels, expert_front(): pl.pallas_call(partial(expert_front_kernel, count), grid=(cols // tile,),...  17.7 us
    unnamed x216, local copies, waits for them, and re-layouts  17.5 us
  transfers between devices with their start and end apart: 28, of which 9 were waited for; matrix products, arithmetic and copies ran while one was open for 18% of the time, Pallas kernels for 49%

profile of v1, /device:TPU:5, one launch (start us, length us, event | category | flops | bytes accessed | tf_op | source)
XLA Modules:
  0.0 705.5 jit_solution(14766238604997934959)
XLA Ops:
  22.3 52.6 %shard_map.590 = (bf16[8,128,1024]{2,1,0:T(8,128)(2,1)S(1)}, bf16[4,8,112,256]{3,2,1,0:T(8,128)(2,1)S(1)}) custom-call(bf16[2,128,1024]{2,1,0:T(8,128)(2,1)S(1)} %bitcast.288, bf16[4,112,256]{2,1,0:T(8,128)(2,1)S(1)} %pad_maximum_fusion.2.col_ref), custom_call_target="tpu_custom_call" | custom-call | bytes 6029312 | tf_op jit(solution)/shard_map/pallas_call | solution.py:79
  79.7 12.2 %collective-permute-start.1 = (bf16[2,128,2816]{2,1,0:T(8,128)(2,1)}, bf16[2,128,2816]{2,1,0:T(8,128)(2,1)}, u32[]{:S(2)}, u32[]{:S(2)}) collective-permute-start(bf16[2,128,2816]{2,1,0:T(8,128)(2,1)} %broadcast_select_fusion.3.refs_0_), channel_id=1, source_target_pairs={{0,8},{1,9},{2,10},{3,11},{4,12},{5,13},{6,14},{7,15},{8,16},{9,17... | collective-permute-start | bytes 4325384 | tf_op jit(solution)/shard_map/ppermute | solution.py:287
  99.7 5.2 attend.1
  105.8 14.2 %collective-permute-done.2 = bf16[2,128,2816]{2,1,0:T(8,128)(2,1)} collective-permute-done((bf16[2,128,2816]{2,1,0:T(8,128)(2,1)}, bf16[2,128,2816]{2,1,0:T(8,128)(2,1)}, u32[]{:S(2)}, u32[]{:S(2)}) %collective-permute-start.2) | collective-permute-done | bytes 1441824 | tf_op jit(solution)/shard_map/ppermute | solution.py:287
  121.7 13.7 %shard_map.591 = bf16[8,128,256]{2,1,0:T(8,128)(2,1)S(1)} custom-call(bf16[8,128,256]{2,1,0:T(8,128)(2,1)S(1)} %bitcast.302), custom_call_target="tpu_custom_call" | custom-call | bytes 4194304 | tf_op jit(solution)/shard_map/pallas_call | solution.py:79
  143.8 30.2 %collective-permute-done.4 = bf16[2,128,2816]{2,1,0:T(8,128)(2,1)} collective-permute-done((bf16[2,128,2816]{2,1,0:T(8,128)(2,1)}, bf16[2,128,2816]{2,1,0:T(8,128)(2,1)}, u32[]{:S(2)}, u32[]{:S(2)}) %collective-permute-start.4) | collective-permute-done | bytes 1441824 | tf_op jit(solution)/shard_map/ppermute | solution.py:287
  188.4 76.6 %collective-permute-done.10 = bf16[2,128,2816]{2,1,0:T(8,128)(2,1)S(1)} collective-permute-done((bf16[2,128,2816]{2,1,0:T(8,128)(2,1)}, bf16[2,128,2816]{2,1,0:T(8,128)(2,1)S(1)}, u32[]{:S(2)}, u32[]{:S(2)}) %collective-permute-start.10) | collective-permute-done | bytes 1441824 | tf_op jit(solution)/shard_map/ppermute | solution.py:287
  268.6 34.6 %shard_map.592 = (bf16[4,2,80,1024]{3,2,1,0:T(8,128)(2,1)S(1)}, bf16[4,2,80,1024]{3,2,1,0:T(8,128)(2,1)S(1)}) custom-call(bf16[4,2,80,1024]{3,2,1,0:T(8,128)(2,1)S(1)} %bitcast.297, bf16[4,2,80,1024]{3,2,1,0:T(8,128)(2,1)S(1)} %bitcast.300), custom_call_target="tpu_custom_call" | custom-call | bytes 20971520 | tf_op jit(solution)/shard_map/pallas_call | solution.py:79
  304.9 17.7 %expert_front.1 = (bf16[640,2816]{1,0:T(8,128)(2,1)}, bf16[640,2816]{1,0:T(8,128)(2,1)}, bf16[640,2816]{1,0:T(8,128)(2,1)}) custom-call(bf16[640,1024]{1,0:T(8,128)(2,1)S(1)} %bitcast.305, bf16[2,128,2816]{2,1,0:T(8,128)(2,1)} %broadcast_select_fusion.3.refs_0_, bf16[2,128,2816]{2,1,0:T(8,128)(2,1)} %collective-permute-done.6.refs_1_, ...), custom_call_target="tpu_custom_call" | custom-call | flops 7381975040 | bytes 11534336 | tf_op jit(solution)/shard_map/expert_front/pallas_call | solution.py:367
  322.7 7.0 convolution_convert_fusion
  333.6 5.1 collective-permute-done.21
  338.8 5.8 fusion
  351.1 12.6 %expert_middle.1 = (bf16[640,2816]{1,0:T(8,128)(2,1)S(1)}, bf16[640,2816]{1,0:T(8,128)(2,1)}) custom-call(bf16[640,1024]{1,0:T(8,128)(2,1)S(1)} %bitcast.296, bf16[2816,1024]{1,0:T(8,128)(2,1)} %bitcast.308, bf16[640,2816]{1,0:T(8,128)(2,1)} %get-tuple-element.91.value_ref, bf16[640,2816]{1,0:T(8,128)(2,1)} %get-tuple-element.92.slope_ref), custom_call_target="tpu_custom_call" | custom-call | flops 3690987520 | bytes 5767168 | tf_op jit(solution)/shard_map/expert_middle/pallas_call | solution.py:392
  371.7 5.1 convolution_convert_fusion.1
  388.9 15.4 %expert_rear.1 = bf16[640,1024]{1,0:T(8,128)(2,1)S(1)} custom-call(bf16[640,2816]{1,0:T(8,128)(2,1)} %copy-done.9, bf16[640,2816]{1,0:T(8,128)(2,1)} %get-tuple-element.94.up_ref, bf16[2,128,2816]{2,1,0:T(8,128)(2,1)} %broadcast_select_fusion.3.refs_0_, bf16[2,128,2816]{2,1,0:T(8,128)(2,1)} %collective-permute-done.6.refs_1_, ...), custom_call_target="tpu_custom_call" | custom-call | flops 7381975040 | bytes 11534336 | tf_op jit(solution)/shard_map/expert_rear/pallas_call | solution.py:439
  404.3 32.6 %shard_map.593 = (bf16[4,2,80,1024]{3,2,1,0:T(8,128)(2,1)S(1)}, bf16[4,2,80,1024]{3,2,1,0:T(8,128)(2,1)S(1)}) custom-call(bf16[4,2,80,1024]{3,2,1,0:T(8,128)(2,1)S(1)} %bitcast.298, bf16[4,2,80,1024]{3,2,1,0:T(8,128)(2,1)S(1)} %bitcast.299), custom_call_target="tpu_custom_call" | custom-call | bytes 20971520 | tf_op jit(solution)/shard_map/pallas_call | solution.py:79
  444.7 21.9 %shard_map.594 = bf16[8,128,256]{2,1,0:T(8,128)(2,1)S(1)} custom-call(bf16[8,128,256]{2,1,0:T(8,128)(2,1)S(1)} %bitcast.294), custom_call_target="tpu_custom_call" | custom-call | bytes 4194304 | tf_op jit(solution)/shard_map/pallas_call | solution.py:79
  467.4 25.1 %attend_back.1 = (bf16[3,1024,256]{2,1,0:T(8,128)(2,1)}, f32[2,8,512]{2,1,0:T(8,128)}) custom-call(bf16[3,1024,256]{2,1,0:T(8,128)(2,1)} %copy-done.12, f32[2,2,2048]{2,1,0:T(2,128)} %copy-done.8, bf16[1024,256]{1,0:T(8,128)(2,1)} %bitcast.303, f32[1024,256]{1,0:T(8,128)} %copy-done.13, f32[1024,256]{1,0:T(8,128)} %copy-done.14), custom_call_target="tpu_custom_call" | custom-call | flops 2684354560 | bytes 7864320 | tf_op jit(solution)/shard_map/attend_back/pallas_call | solution.py:635
  517.3 74.6 %shard_map.595 = bf16[8,128,1024]{2,1,0:T(8,128)(2,1)S(1)} custom-call(bf16[8,128,1024]{2,1,0:T(8,128)(2,1)S(1)} %bitcast.292), custom_call_target="tpu_custom_call" | custom-call | bytes 16777216 | tf_op jit(solution)/shard_map/pallas_call | solution.py:79
  600.7 5.3 collective-permute-done.14
  606.2 11.0 %collective-permute-done.16 = bf16[8,32,1024]{2,1,0:T(8,128)(2,1)S(1)} collective-permute-done((bf16[8,32,1024]{2,1,0:T(8,128)(2,1)S(1)}, bf16[8,32,1024]{2,1,0:T(8,128)(2,1)S(1)}, u32[]{:S(2)}, u32[]{:S(2)}) %collective-permute-start.16) | collective-permute-done | bytes 524320 | tf_op jit(solution)/shard_map/ppermute | solution.py:36
  617.4 38.3 %shard_map.596 = (bf16[8,3,32,256]{3,2,1,0:T(8,128)(2,1)S(1)}, bf16[8,32,1024]{2,1,0:T(8,128)(2,1)S(1)}, f32[8,4,1,256]{3,2,1,0:T(1,128)}, f32[4,8,4,1,256]{4,3,2,1,0:T(1,128)S(1)}) custom-call(bf16[8,3,32,256]{3,2,1,0:T(8,128)(2,1)S(1)} %fusion.46.col_ref, bf16[8,32,1024]{2,1,0:T(8,128)(2,1)S(1)} %fusion.38.out_in, f32[8,4,1,256]{3,2,1,0:T(1,128)S(1)} %reshape.458.small_ref), custom_call_target="tpu_custom_call" | custom-call | bytes 7602176 | tf_op jit(solution)/shard_map/pallas_call | solution.py:79
  658.0 7.7 %collective-permute-start.22 = (bf16[352,1024]{1,0:T(8,128)(2,1)}, bf16[352,1024]{1,0:T(8,128)(2,1)}, u32[]{:S(2)}, u32[]{:S(2)}) collective-permute-start(bf16[352,1024]{1,0:T(8,128)(2,1)} %bitcast.336), channel_id=1, source_target_pairs={{1,4},{3,6},{4,1},{6,3},{9,12},{11,14},{12,9},{14,11},{17,20},{19,... | collective-permute-start | bytes 2162696 | tf_op jit(solution)/shard_map/ppermute | solution.py:54
  675.0 5.3 add_multiply_fusion
  (415 shorter events, 159.5 us)
Async XLA Ops:
  7.2 132.1 %all-gather.4.cloned.1.call-start = ((), (), s32[]{:S(2)}) async-start(), calls=%async_computation.3 | async-start | bytes 2162688 | tf_op jit(solution)/shard_map/all_gather | solution.py:714
  10.5 64.5 %collective-permute-start = (bf16[2,128,2816]{2,1,0:T(8,128)(2,1)}, bf16[2,128,2816]{2,1,0:T(8,128)(2,1)}, u32[]{:S(2)}, u32[]{:S(2)}) collective-permute-start(bf16[2,128,2816]{2,1,0:T(8,128)(2,1)} %pad_maximum_fusion.1), channel_id=1, source_target_pairs={{1,4},{3,6},{4,1},{6,3},{9,12},{11,14},{12,9},{14,11},{17,20},{19,... | collective-permute-start | bytes 4325384 | tf_op jit(solution)/shard_map/ppermute | solution.py:54
  15.0 318.2 %all-gather.6.cloned.1.call-start = ((), (), s32[]{:S(2)}) async-start(), calls=%async_computation.7 | async-start | bytes 3604480 | tf_op jit(solution)/shard_map/all_gather | solution.py:303
  16.0 161.0 %collective-permute-start.5 = (bf16[352,1024]{1,0:T(8,128)(2,1)}, bf16[352,1024]{1,0:T(8,128)(2,1)}, u32[]{:S(2)}, u32[]{:S(2)}) collective-permute-start(bf16[352,1024]{1,0:T(8,128)(2,1)} %convert_bitcast_fusion.3), channel_id=1, source_target_pairs={{1,4},{3,6},{4,1},{6,3},{9,12},{11,14},{12,9},{14,11},{17,20},{19,... | collective-permute-start | bytes 2162696 | tf_op jit(solution)/shard_map/ppermute | solution.py:54
  78.5 41.5 %collective-permute-start.2 = (bf16[2,128,2816]{2,1,0:T(8,128)(2,1)}, bf16[2,128,2816]{2,1,0:T(8,128)(2,1)}, u32[]{:S(2)}, u32[]{:S(2)}) collective-permute-start(bf16[2,128,2816]{2,1,0:T(8,128)(2,1)} %broadcast_select_fusion.3.refs_0_), channel_id=1, source_target_pairs={{8,0},{9,1},{10,2},{11,3},{12,4},{13,5},{14,6},{15,7},{16,8},{17,9... | collective-permute-start | bytes 4325384 | tf_op jit(solution)/shard_map/ppermute | solution.py:287
  79.7 42.0 %collective-permute-start.1 = (bf16[2,128,2816]{2,1,0:T(8,128)(2,1)}, bf16[2,128,2816]{2,1,0:T(8,128)(2,1)}, u32[]{:S(2)}, u32[]{:S(2)}) collective-permute-start(bf16[2,128,2816]{2,1,0:T(8,128)(2,1)} %broadcast_select_fusion.3.refs_0_), channel_id=1, source_target_pairs={{0,8},{1,9},{2,10},{3,11},{4,12},{5,13},{6,14},{7,15},{8,16},{9,17... | collective-permute-start | bytes 4325384 | tf_op jit(solution)/shard_map/ppermute | solution.py:287
  137.3 36.7 %collective-permute-start.4 = (bf16[2,128,2816]{2,1,0:T(8,128)(2,1)}, bf16[2,128,2816]{2,1,0:T(8,128)(2,1)}, u32[]{:S(2)}, u32[]{:S(2)}) collective-permute-start(bf16[2,128,2816]{2,1,0:T(8,128)(2,1)} %collective-permute-done.2), channel_id=1, source_target_pairs={{8,0},{9,1},{10,2},{11,3},{12,4},{13,5},{14,6},{15,7},{16,8},{17,9... | collective-permute-start | bytes 4325384 | tf_op jit(solution)/shard_map/ppermute | solution.py:287
  174.0 12.3 %collective-permute-start.7 = (bf16[2,128,2816]{2,1,0:T(8,128)(2,1)}, bf16[2,128,2816]{2,1,0:T(8,128)(2,1)}, u32[]{:S(2)}, u32[]{:S(2)}) collective-permute-start(bf16[2,128,2816]{2,1,0:T(8,128)(2,1)} %collective-permute-done.3), channel_id=1, source_target_pairs={{16,24},{17,25},{18,26},{19,27},{20,28},{21,29},{22,30},{23,31}} | collective-permute-start | bytes 4325384 | tf_op jit(solution)/shard_map/ppermute | solution.py:287
  179.6 123.7 %collective-permute-start.6 = (bf16[2,128,2816]{2,1,0:T(8,128)(2,1)}, bf16[2,128,2816]{2,1,0:T(8,128)(2,1)}, u32[]{:S(2)}, u32[]{:S(2)}) collective-permute-start(bf16[2,128,2816]{2,1,0:T(8,128)(2,1)} %broadcast_select_fusion.3.refs_0_), channel_id=1, source_target_pairs={{0,1},{1,0},{2,3},{3,2},{4,5},{5,4},{6,7},{7,6},{8,9},{9,8},{10,11... | collective-permute-start | bytes 4325384 | tf_op jit(solution)/shard_map/ppermute | solution.py:36
  183.3 474.7 %reduce-scatter.8.cloned.1.call-start = ((), (), s32[]{:S(2)}) async-start(), calls=%async_computation.6 | async-start | bytes 3604480 | tf_op jit(solution)/shard_map/reduce_scatter | solution.py:320
  183.4 81.7 %collective-permute-start.10 = (bf16[2,128,2816]{2,1,0:T(8,128)(2,1)}, bf16[2,128,2816]{2,1,0:T(8,128)(2,1)S(1)}, u32[]{:S(2)}, u32[]{:S(2)}) collective-permute-start(bf16[2,128,2816]{2,1,0:T(8,128)(2,1)} %collective-permute-done.4), channel_id=1, source_target_pairs={{8,0},{9,1},{10,2},{11,3},{12,4},{13,5},{14,6},{15,7}} | collective-permute-start | bytes 4325384 | tf_op jit(solution)/shard_map/ppermute | solution.py:287
  186.2 117.1 %collective-permute-start.9 = (bf16[2,128,2816]{2,1,0:T(8,128)(2,1)S(1)}, bf16[2,128,2816]{2,1,0:T(8,128)(2,1)S(1)}, u32[]{:S(2)}, u32[]{:S(2)}) collective-permute-start(bf16[2,128,2816]{2,1,0:T(8,128)(2,1)S(1)} %broadcast_select_fusion.1.refs_4_), channel_id=1, source_target_pairs={{0,1},{1,0},{2,3},{3,2},{4,5},{5,4},{6,7},{7,6},{8,9},{9,8},{10,11... | collective-permute-start | bytes 4325384 | tf_op jit(solution)/shard_map/ppermute | solution.py:36
  188.3 115.0 %collective-permute-start.8 = (bf16[2,128,2816]{2,1,0:T(8,128)(2,1)S(1)}, bf16[2,128,2816]{2,1,0:T(8,128)(2,1)}, u32[]{:S(2)}, u32[]{:S(2)}) collective-permute-start(bf16[2,128,2816]{2,1,0:T(8,128)(2,1)S(1)} %broadcast_select_fusion.2.refs_2_), channel_id=1, source_target_pairs={{0,1},{1,0},{2,3},{3,2},{4,5},{5,4},{6,7},{7,6},{8,9},{9,8},{10,11... | collective-permute-start | bytes 4325384 | tf_op jit(solution)/shard_map/ppermute | solution.py:36
  265.2 38.1 %collective-permute-start.11 = (bf16[2,128,2816]{2,1,0:T(8,128)(2,1)S(1)}, bf16[2,128,2816]{2,1,0:T(8,128)(2,1)S(1)}, u32[]{:S(2)}, u32[]{:S(2)}) collective-permute-start(bf16[2,128,2816]{2,1,0:T(8,128)(2,1)S(1)} %broadcast_select_fusion.refs_6_), channel_id=1, source_target_pairs={{0,1},{1,0},{2,3},{3,2},{4,5},{5,4},{6,7},{7,6},{8,9},{9,8},{10,11... | collective-permute-start | bytes 4325384 | tf_op jit(solution)/shard_map/ppermute | solution.py:36
  344.5 324.0 %reduce-scatter.4.cloned.1.call-start = ((), (), s32[]{:S(2)}) async-start(), calls=%async_computation.4 | async-start | bytes 3604480 | tf_op jit(solution)/shard_map/reduce_scatter | solution.py:320
  368.8 16.5 %collective-permute-start.17 = (bf16[4,128,2816]{2,1,0:T(8,128)(2,1)S(1)}, bf16[4,128,2816]{2,1,0:T(8,128)(2,1)S(1)}, u32[]{:S(2)}, u32[]{:S(2)}) collective-permute-start(bf16[4,128,2816]{2,1,0:T(8,128)(2,1)S(1)} %dynamic-slice_bitcast_fusion.2), channel_id=1, source_target_pairs={{0,1},{1,0},{2,3},{3,2},{4,5},{5,4},{6,7},{7,6},{8,9},{9,8},{10,11... | collective-permute-start | bytes 8650760 | tf_op jit(solution)/shard_map/ppermute | solution.py:36
  380.9 125.4 %collective-permute-start.19 = (bf16[4,128,2816]{2,1,0:T(8,128)(2,1)}, bf16[4,128,2816]{2,1,0:T(8,128)(2,1)}, u32[]{:S(2)}, u32[]{:S(2)}) collective-permute-start(bf16[4,128,2816]{2,1,0:T(8,128)(2,1)} %dynamic-slice_bitcast_fusion.1), channel_id=1, source_target_pairs={{0,1},{1,0},{2,3},{3,2},{4,5},{5,4},{6,7},{7,6},{8,9},{9,8},{10,11... | collective-permute-start | bytes 8650760 | tf_op jit(solution)/shard_map/ppermute | solution.py:36
  387.6 294.0 %reduce-scatter.6.cloned.1.call-start = ((), (), s32[]{:S(2)}) async-start(), calls=%async_computation.5 | async-start | bytes 3604480 | tf_op jit(solution)/shard_map/reduce_scatter | solution.py:320
  502.3 92.1 %collective-permute-start.13 = (bf16[2,8,3,32,256]{4,3,2,1,0:T(8,128)(2,1)}, bf16[2,8,3,32,256]{4,3,2,1,0:T(8,128)(2,1)}, u32[]{:S(2)}, u32[]{:S(2)}) collective-permute-start(bf16[2,8,3,32,256]{4,3,2,1,0:T(8,128)(2,1)} %bitcast.281), channel_id=1, source_target_pairs={{0,1},{1,0},{2,3},{3,2},{4,5},{5,4},{6,7},{7,6},{8,9},{9,8},{10,11... | collective-permute-start | bytes 2359304 | tf_op jit(solution)/shard_map/ppermute | solution.py:36
  506.2 90.1 %collective-permute-start.15 = (bf16[2,8,32,1024]{3,2,1,0:T(8,128)(2,1)}, bf16[2,8,32,1024]{3,2,1,0:T(8,128)(2,1)}, u32[]{:S(2)}, u32[]{:S(2)}) collective-permute-start(bf16[2,8,32,1024]{3,2,1,0:T(8,128)(2,1)} %bitcast.280), channel_id=1, source_target_pairs={{0,1},{1,0},{2,3},{3,2},{4,5},{5,4},{6,7},{7,6},{8,9},{9,8},{10,11... | collective-permute-start | bytes 3145736 | tf_op jit(solution)/shard_map/ppermute | solution.py:36
  598.0 19.2 %collective-permute-start.16 = (bf16[8,32,1024]{2,1,0:T(8,128)(2,1)S(1)}, bf16[8,32,1024]{2,1,0:T(8,128)(2,1)S(1)}, u32[]{:S(2)}, u32[]{:S(2)}) collective-permute-start(bf16[8,32,1024]{2,1,0:T(8,128)(2,1)S(1)} %dynamic-slice_bitcast_fusion.3), channel_id=1, source_target_pairs={{0,2},{1,3},{2,0},{3,1},{4,6},{5,7},{6,4},{7,5},{8,10},{9,11},{10,... | collective-permute-start | bytes 1572872 | tf_op jit(solution)/shard_map/ppermute | solution.py:36
  658.0 17.0 %collective-permute-start.22 = (bf16[352,1024]{1,0:T(8,128)(2,1)}, bf16[352,1024]{1,0:T(8,128)(2,1)}, u32[]{:S(2)}, u32[]{:S(2)}) collective-permute-start(bf16[352,1024]{1,0:T(8,128)(2,1)} %bitcast.336), channel_id=1, source_target_pairs={{1,4},{3,6},{4,1},{6,3},{9,12},{11,14},{12,9},{14,11},{17,20},{19,... | collective-permute-start | bytes 2162696 | tf_op jit(solution)/shard_map/ppermute | solution.py:54
  668.5 16.9 %collective-permute-start.18 = (bf16[128,2816]{1,0:T(8,128)(2,1)}, bf16[128,2816]{1,0:T(8,128)(2,1)}, u32[]{:S(2)}, u32[]{:S(2)}) collective-permute-start(bf16[128,2816]{1,0:T(8,128)(2,1)} %bitcast.337), channel_id=1, source_target_pairs={{1,4},{3,6},{4,1},{6,3},{9,12},{11,14},{12,9},{14,11},{17,20},{19,... | collective-permute-start | bytes 2162696 | tf_op jit(solution)/shard_map/ppermute | solution.py:54
  681.6 12.8 %collective-permute-start.20 = (bf16[128,2816]{1,0:T(8,128)(2,1)}, bf16[128,2816]{1,0:T(8,128)(2,1)S(1)}, u32[]{:S(2)}, u32[]{:S(2)}) collective-permute-start(bf16[128,2816]{1,0:T(8,128)(2,1)} %bitcast.338), channel_id=1, source_target_pairs={{1,4},{3,6},{4,1},{6,3},{9,12},{11,14},{12,9},{14,11},{17,20},{19,... | collective-permute-start | bytes 2162696 | tf_op jit(solution)/shard_map/ppermute | solution.py:54
  (107 other events, 1552.4 us)
Sparse Core Ops, SparseCore 0:
  15.1 69.3 all-gather.3
  183.4 81.5 all-gather.5
  344.7 53.8 reduce-scatter.7
  400.7 62.0 reduce-scatter.3
  510.6 88.3 reduce-scatter.5

commit v2 on v1

--- a/solution.py
+++ b/solution.py
@@ -714,8 +714,6 @@
     w_out = lax.all_gather(out_master.astype(bf16), both, axis=0, tiled=True)
     pair_own = turn(jnp.concatenate([gate_master, up_master], axis=0).astype(bf16))
     down_own = turn(down_master[0].astype(bf16))
-    seq, gathered = opening(tok, cols)
-    pair_own, seq, gathered = lax.optimization_barrier((pair_own, seq, gathered))
     right, left = [pair_own], [pair_own]
 
     def line_round(step):
@@ -727,6 +725,9 @@
         return value
 
     line_round(0)
+    seq, gathered = opening(tok, cols)
+    seq = line_settle(seq)
+    line_round(1)
     seq = seq.reshape(length, D)
     w_qkv = gathered[:, :, : 3 * rows].reshape(EXP_AXIS, cycle, 3, rows, width)
     w_qkv = w_qkv.transpose(2, 1, 0, 3, 4).reshape(3, D, width)
@@ -753,10 +754,10 @@
     qkv = jnp.einsum("td,cde->cte", normed, w_qkv, preferred_element_type=f32).astype(bf16)
     attended, summed, total = attend(qkv, offset_bias)
 
-    attended = line_settle(attended)
     back = cycle_swap(attended.reshape(cycle, tok_rows, width), 1)
     back = line_settle(back)
-    line_round(1)
+    if line > 3:
+        line_round(2)
     toks = micro * tok_rows
     attended_bf = back.reshape(micro, group, tok_rows, width).transpose(0, 2, 1, 3)
     attended_bf = attended_bf.reshape(toks, D)
@@ -793,12 +794,10 @@
         jnp.concatenate(hits, axis=0), jnp.concatenate(scaled_dy, axis=0), first_dims,
         preferred_element_type=f32,
     )
-    sent_rows, down_own = lax.optimization_barrier((line_settle(sent_rows.astype(bf16)), down_own))
-    if line > 3:
-        line_round(2)
-    got_rows, got_grads = plane_swap(
-        (sent_rows.reshape(slots), sent_grads.astype(bf16).reshape(slots)), True, 2
-    )
+    sent_rows = sent_rows.astype(bf16)
+    sent_grads = line_settle(sent_grads.astype(bf16))
+    sent_grads, down_own = lax.optimization_barrier((sent_grads, down_own))
+    got_rows, got_grads = plane_swap((sent_rows.reshape(slots), sent_grads.reshape(slots)), True, 2)
     for step in range(3, line - 1):
         line_round(step)
     flat_rows = got_rows.reshape(-1, D)
@@ -881,14 +880,14 @@
     out_grad = cube_sum(out_grad, 1)
 
     dqkv, diag = attend_back(qkv, offset_bias, grad_attended, summed, total)
+    partial_normed = jnp.einsum("cte,cde->td", dqkv, w_qkv, preferred_element_type=f32)
+    partial_normed = partial_normed.astype(bf16).reshape(cycle, tok_rows, D)
+    pieces = lax.all_to_all(partial_normed, "ctx", 0, 0, tiled=True)
     qkv_grad = jnp.einsum("td,cte->cde", normed, dqkv, preferred_element_type=f32)
     qkv_grad = qkv_grad.astype(bf16).reshape(3, cycle, 2, 2, rows, width)
     qkv_grad = qkv_grad.transpose(3, 2, 1, 0, 4, 5)
     qkv_grad = cube_sum(qkv_grad, 0)
     qkv_grad = cube_sum(qkv_grad, 1)
-    partial_normed = jnp.einsum("cte,cde->td", dqkv, w_qkv, preferred_element_type=f32)
-    partial_normed = partial_normed.astype(bf16).reshape(cycle, tok_rows, D)
-    pieces = cycle_swap(partial_normed, 5)
     grad_normed_attn = jnp.sum(pieces.reshape(micro, group, tok_rows, D).astype(f32), axis=1)
     grad_inputs, gain_attn_grad = norm_back(
         inputs, factor_attn, gain_attn, grad_normed_attn.reshape(toks, D)

time: 717 us -> 621 us (0.87)
  Pallas kernels: 344 us -> 276 us
  waiting for transfers between devices: 152 us -> 99 us
  other arithmetic: 67.3 us -> 78.3 us
    ppermute x6, waiting for transfers between devices: 123 us -> 44.9 us  [line_permute(): return lax.ppermute(value, both, pairs)]
    pallas_call x7 -> x6, Pallas kernels: 268 us -> 198 us  [exchange_call(): pl.pallas_call(kernel, in_specs=[vmem] * len(arrays), out_specs=[vmem] *...]
    all_to_all x0 -> x1, waiting for transfers between devices: none -> 33.6 us  [layer(): pieces = lax.all_to_all(partial_normed, 'ctx', 0, 0, tiled=True)]
    unnamed x216 -> x248, local copies, waits for them, and re-layouts: 17.5 us -> 20.5 us
  transfers between devices with their start and end apart: 28 -> 29, of which waited for: 9 -> 9; matrix products, arithmetic and copies ran while one was open for 18% -> 24% of each run, Pallas kernels for 49% -> 45%
where the time goes in v2:
time: 621 us; the launch traced here: 610 us
  Pallas kernels  276 us (44%)
  waiting for transfers between devices  99 us (16%)
  other arithmetic  78.3 us (13%)
  starting transfers between devices  51.8 us (8%)
  matrix products  48.6 us (8%)
  local copies, waits for them, and re-layouts  40.8 us (7%)
  between operations  16.2 us (3%)
    pallas_call x6, Pallas kernels, exchange_call(): pl.pallas_call(kernel, in_specs=[vmem] * len(arrays), out_specs=[vmem] *...  198 us
    ppermute x6, waiting for transfers between devices, line_permute(): return lax.ppermute(value, both, pairs)  44.9 us
    all_to_all x1, waiting for transfers between devices, layer(): pieces = lax.all_to_all(partial_normed, 'ctx', 0, 0, tiled=True)  33.6 us
    pallas_call x1, Pallas kernels, attend_back(): pl.pallas_call(partial(attend_back_kernel, blocks, heads), grid=(steps,),...  25.2 us
    unnamed x248, local copies, waits for them, and re-layouts  20.5 us
    ppermute x6, starting transfers between devices, line_permute(): return lax.ppermute(value, both, pairs)  19.8 us
    pallas_call x1, Pallas kernels, expert_front(): pl.pallas_call(partial(expert_front_kernel, count), grid=(cols // tile,),...  18.6 us
    ppermute x5, starting transfers between devices, turn(): lax.ppermute(value, both, [(d, other(d)) for d in range(count) if other(d...  17.4 us
  transfers between devices with their start and end apart: 29, of which 9 were waited for; matrix products, arithmetic and copies ran while one was open for 24% of the time, Pallas kernels for 45%

profile of v2, /device:TPU:5, one launch (start us, length us, event | category | flops | bytes accessed | tf_op | source)
XLA Modules:
  0.0 610.3 jit_solution(4899620095534092245)
XLA Ops:
  22.2 53.0 %shard_map.590 = (bf16[8,128,1024]{2,1,0:T(8,128)(2,1)S(1)}, bf16[4,8,112,256]{3,2,1,0:T(8,128)(2,1)S(1)}) custom-call(bf16[2,128,1024]{2,1,0:T(8,128)(2,1)S(1)} %bitcast.288, bf16[4,112,256]{2,1,0:T(8,128)(2,1)S(1)} %pad_maximum_fusion.2.col_ref), custom_call_target="tpu_custom_call" | custom-call | bytes 6029312 | tf_op jit(solution)/shard_map/pallas_call | solution.py:79
  81.2 12.1 %collective-permute-start.1 = (bf16[2,128,2816]{2,1,0:T(8,128)(2,1)}, bf16[2,128,2816]{2,1,0:T(8,128)(2,1)}, u32[]{:S(2)}, u32[]{:S(2)}) collective-permute-start(bf16[2,128,2816]{2,1,0:T(8,128)(2,1)} %broadcast_select_fusion.3.refs_0_), channel_id=1, source_target_pairs={{0,8},{1,9},{2,10},{3,11},{4,12},{5,13},{6,14},{7,15},{8,16},{9,17... | collective-permute-start | bytes 4325384 | tf_op jit(solution)/shard_map/ppermute | solution.py:287
  101.4 20.2 %collective-permute-done.2 = bf16[2,128,2816]{2,1,0:T(8,128)(2,1)} collective-permute-done((bf16[2,128,2816]{2,1,0:T(8,128)(2,1)}, bf16[2,128,2816]{2,1,0:T(8,128)(2,1)}, u32[]{:S(2)}, u32[]{:S(2)}) %collective-permute-start.2) | collective-permute-done | bytes 1441824 | tf_op jit(solution)/shard_map/ppermute | solution.py:287
  133.4 5.2 attend.1
  138.7 32.9 %shard_map.591 = bf16[8,128,256]{2,1,0:T(8,128)(2,1)S(1)} custom-call(bf16[8,128,256]{2,1,0:T(8,128)(2,1)S(1)} %bitcast.302), custom_call_target="tpu_custom_call" | custom-call | bytes 4194304 | tf_op jit(solution)/shard_map/pallas_call | solution.py:79
  187.7 22.9 %collective-permute-done.6 = bf16[2,128,2816]{2,1,0:T(8,128)(2,1)} collective-permute-done((bf16[2,128,2816]{2,1,0:T(8,128)(2,1)}, bf16[2,128,2816]{2,1,0:T(8,128)(2,1)}, u32[]{:S(2)}, u32[]{:S(2)}) %collective-permute-start.6) | collective-permute-done | bytes 1441824 | tf_op jit(solution)/shard_map/ppermute | solution.py:287
  220.7 34.2 %shard_map.592 = (bf16[4,2,80,1024]{3,2,1,0:T(8,128)(2,1)S(1)}, bf16[4,2,80,1024]{3,2,1,0:T(8,128)(2,1)S(1)}) custom-call(bf16[4,2,80,1024]{3,2,1,0:T(8,128)(2,1)S(1)} %bitcast.299, bf16[4,2,80,1024]{3,2,1,0:T(8,128)(2,1)S(1)} %bitcast.296), custom_call_target="tpu_custom_call" | custom-call | bytes 20971520 | tf_op jit(solution)/shard_map/pallas_call | solution.py:79
  254.9 18.6 %expert_front.1 = (bf16[640,2816]{1,0:T(8,128)(2,1)}, bf16[640,2816]{1,0:T(8,128)(2,1)}, bf16[640,2816]{1,0:T(8,128)(2,1)}) custom-call(bf16[640,1024]{1,0:T(8,128)(2,1)S(1)} %bitcast.304, bf16[2,128,2816]{2,1,0:T(8,128)(2,1)} %broadcast_select_fusion.3.refs_0_, bf16[2,128,2816]{2,1,0:T(8,128)(2,1)} %collective-permute-done.8.refs_1_, ...), custom_call_target="tpu_custom_call" | custom-call | flops 7381975040 | bytes 11534336 | tf_op jit(solution)/shard_map/expert_front/pallas_call | solution.py:367
  273.6 7.0 %convolution_convert_fusion = bf16[2816,1024]{1,0:T(8,128)(2,1)S(1)} fusion(bf16[640,2816]{1,0:T(8,128)(2,1)} %get-tuple-element.82, bf16[640,1024]{1,0:T(8,128)(2,1)S(1)} %bitcast.294), kind=kOutput, calls=%fused_computation.7 | convolution fusion | flops 3693871104 | bytes 10682368 | tf_op jit(solution)/shard_map/dot_general | solution.py:834
  284.4 5.1 collective-permute-done.21
  289.5 5.7 fusion
  301.8 12.6 %expert_middle.1 = (bf16[640,2816]{1,0:T(8,128)(2,1)S(1)}, bf16[640,2816]{1,0:T(8,128)(2,1)}) custom-call(bf16[640,1024]{1,0:T(8,128)(2,1)S(1)} %bitcast.295, bf16[2816,1024]{1,0:T(8,128)(2,1)} %bitcast.307, bf16[640,2816]{1,0:T(8,128)(2,1)} %get-tuple-element.85.value_ref, bf16[640,2816]{1,0:T(8,128)(2,1)} %get-tuple-element.86.slope_ref), custom_call_target="tpu_custom_call" | custom-call | flops 3690987520 | bytes 5767168 | tf_op jit(solution)/shard_map/expert_middle/pallas_call | solution.py:392
  325.5 7.5 %convolution_convert_fusion.1 = bf16[1024,2816]{1,0:T(8,128)(2,1)S(1)} fusion(bf16[640,1024]{1,0:T(8,128)(2,1)S(1)} %bitcast.306, bf16[640,2816]{1,0:T(8,128)(2,1)} %get-tuple-element.88.up_ref), kind=kOutput, calls=%fused_computation.8 | convolution fusion | flops 3693871104 | bytes 10682368 | tf_op jit(solution)/shard_map/dot_general | solution.py:837
  345.8 16.1 %expert_rear.1 = bf16[640,1024]{1,0:T(8,128)(2,1)S(1)} custom-call(bf16[640,2816]{1,0:T(8,128)(2,1)} %copy-done.7, bf16[640,2816]{1,0:T(8,128)(2,1)} %get-tuple-element.88.up_ref, bf16[2,128,2816]{2,1,0:T(8,128)(2,1)} %broadcast_select_fusion.3.refs_0_, bf16[2,128,2816]{2,1,0:T(8,128)(2,1)} %collective-permute-done.8.refs_1_, ...), custom_call_target="tpu_custom_call" | custom-call | flops 7381975040 | bytes 11534336 | tf_op jit(solution)/shard_map/expert_rear/pallas_call | solution.py:439
  361.9 33.0 %shard_map.593 = (bf16[4,2,80,1024]{3,2,1,0:T(8,128)(2,1)S(1)}, bf16[4,2,80,1024]{3,2,1,0:T(8,128)(2,1)S(1)}) custom-call(bf16[4,2,80,1024]{3,2,1,0:T(8,128)(2,1)S(1)} %bitcast.297, bf16[4,2,80,1024]{3,2,1,0:T(8,128)(2,1)S(1)} %bitcast.298), custom_call_target="tpu_custom_call" | custom-call | bytes 20971520 | tf_op jit(solution)/shard_map/pallas_call | solution.py:79
  402.7 14.9 %shard_map.594 = bf16[8,128,256]{2,1,0:T(8,128)(2,1)S(1)} custom-call(bf16[8,128,256]{2,1,0:T(8,128)(2,1)S(1)} %bitcast.293), custom_call_target="tpu_custom_call" | custom-call | bytes 4194304 | tf_op jit(solution)/shard_map/pallas_call | solution.py:79
  418.4 25.2 %attend_back.1 = (bf16[3,1024,256]{2,1,0:T(8,128)(2,1)}, f32[2,8,512]{2,1,0:T(8,128)}) custom-call(bf16[3,1024,256]{2,1,0:T(8,128)(2,1)} %copy-done.11, f32[2,2,2048]{2,1,0:T(2,128)} %copy-done.6, bf16[1024,256]{1,0:T(8,128)(2,1)} %bitcast.301, f32[1024,256]{1,0:T(8,128)} %copy-done.12, f32[1024,256]{1,0:T(8,128)} %copy-done.13), custom_call_target="tpu_custom_call" | custom-call | flops 2684354560 | bytes 7864320 | tf_op jit(solution)/shard_map/attend_back/pallas_call | solution.py:635
  449.8 5.0 bitcast_convert_fusion
  488.1 10.1 %collective-permute-done.16 = bf16[8,32,1024]{2,1,0:T(8,128)(2,1)} collective-permute-done((bf16[8,32,1024]{2,1,0:T(8,128)(2,1)S(1)}, bf16[8,32,1024]{2,1,0:T(8,128)(2,1)}, u32[]{:S(2)}, u32[]{:S(2)}) %collective-permute-start.16) | collective-permute-done | bytes 524320 | tf_op jit(solution)/shard_map/ppermute | solution.py:36
  499.6 5.2 add_multiply_fusion
  506.1 33.6 %all-to-all-done = bf16[8,128,1024]{2,1,0:T(8,128)(2,1)} async-done(((bf16[8,128,1024]{2,1,0:T(8,128)(2,1)}), bf16[8,128,1024]{2,1,0:T(8,128)(2,1)}, u32[]{:S(2)}, u32[]{:S(2)}) %all-to-all-start) | async-done | bytes 2097184 | tf_op jit(solution)/shard_map/all_to_all | solution.py:885
  543.6 30.1 %shard_map.595 = (bf16[8,3,32,256]{3,2,1,0:T(8,128)(2,1)S(1)}, bf16[8,32,1024]{2,1,0:T(8,128)(2,1)S(1)}, f32[8,4,1,256]{3,2,1,0:T(1,128)}, f32[4,8,4,1,256]{4,3,2,1,0:T(1,128)S(1)}) custom-call(bf16[8,3,32,256]{3,2,1,0:T(8,128)(2,1)S(1)} %fusion.46.col_ref, bf16[8,32,1024]{2,1,0:T(8,128)(2,1)S(1)} %fusion.38.out_in, f32[8,4,1,256]{3,2,1,0:T(1,128)S(1)} %reshape.458.small_ref), custom_call_target="tpu_custom_call" | custom-call | bytes 7602176 | tf_op jit(solution)/shard_map/pallas_call | solution.py:79
  576.9 5.5 collective-permute-start.18
  591.6 5.0 add_multiply_fusion.2
  (450 shorter events, 173.5 us)
Async XLA Ops:
  7.2 165.0 %all-gather.4.cloned.1.call-start = ((), (), s32[]{:S(2)}) async-start(), calls=%async_computation.4 | async-start | bytes 2162688 | tf_op jit(solution)/shard_map/all_gather | solution.py:714
  10.6 66.2 %collective-permute-start = (bf16[2,128,2816]{2,1,0:T(8,128)(2,1)}, bf16[2,128,2816]{2,1,0:T(8,128)(2,1)}, u32[]{:S(2)}, u32[]{:S(2)}) collective-permute-start(bf16[2,128,2816]{2,1,0:T(8,128)(2,1)} %pad_maximum_fusion.1), channel_id=1, source_target_pairs={{1,4},{3,6},{4,1},{6,3},{9,12},{11,14},{12,9},{14,11},{17,20},{19,... | collective-permute-start | bytes 4325384 | tf_op jit(solution)/shard_map/ppermute | solution.py:54
  15.1 269.0 %all-gather.6.cloned.1.call-start = ((), (), s32[]{:S(2)}) async-start(), calls=%async_computation.8 | async-start | bytes 3604480 | tf_op jit(solution)/shard_map/all_gather | solution.py:303
  16.1 110.4 %collective-permute-start.7 = (bf16[352,1024]{1,0:T(8,128)(2,1)}, bf16[352,1024]{1,0:T(8,128)(2,1)}, u32[]{:S(2)}, u32[]{:S(2)}) collective-permute-start(bf16[352,1024]{1,0:T(8,128)(2,1)} %convert_bitcast_fusion.3), channel_id=1, source_target_pairs={{1,4},{3,6},{4,1},{6,3},{9,12},{11,14},{12,9},{14,11},{17,20},{19,... | collective-permute-start | bytes 2162696 | tf_op jit(solution)/shard_map/ppermute | solution.py:54
  79.9 41.8 %collective-permute-start.2 = (bf16[2,128,2816]{2,1,0:T(8,128)(2,1)}, bf16[2,128,2816]{2,1,0:T(8,128)(2,1)}, u32[]{:S(2)}, u32[]{:S(2)}) collective-permute-start(bf16[2,128,2816]{2,1,0:T(8,128)(2,1)} %broadcast_select_fusion.3.refs_0_), channel_id=1, source_target_pairs={{8,0},{9,1},{10,2},{11,3},{12,4},{13,5},{14,6},{15,7},{16,8},{17,9... | collective-permute-start | bytes 4325384 | tf_op jit(solution)/shard_map/ppermute | solution.py:287
  81.2 42.2 %collective-permute-start.1 = (bf16[2,128,2816]{2,1,0:T(8,128)(2,1)}, bf16[2,128,2816]{2,1,0:T(8,128)(2,1)}, u32[]{:S(2)}, u32[]{:S(2)}) collective-permute-start(bf16[2,128,2816]{2,1,0:T(8,128)(2,1)} %broadcast_select_fusion.3.refs_0_), channel_id=1, source_target_pairs={{0,8},{1,9},{2,10},{3,11},{4,12},{5,13},{6,14},{7,15},{8,16},{9,17... | collective-permute-start | bytes 4325384 | tf_op jit(solution)/shard_map/ppermute | solution.py:287
  123.4 48.2 %collective-permute-start.3 = (bf16[2,128,2816]{2,1,0:T(8,128)(2,1)}, bf16[2,128,2816]{2,1,0:T(8,128)(2,1)}, u32[]{:S(2)}, u32[]{:S(2)}) collective-permute-start(bf16[2,128,2816]{2,1,0:T(8,128)(2,1)} %collective-permute-done.1), channel_id=1, source_target_pairs={{8,16},{9,17},{10,18},{11,19},{12,20},{13,21},{14,22},{15,23},{16,... | collective-permute-start | bytes 4325384 | tf_op jit(solution)/shard_map/ppermute | solution.py:287
  125.3 46.3 %collective-permute-start.4 = (bf16[2,128,2816]{2,1,0:T(8,128)(2,1)}, bf16[2,128,2816]{2,1,0:T(8,128)(2,1)}, u32[]{:S(2)}, u32[]{:S(2)}) collective-permute-start(bf16[2,128,2816]{2,1,0:T(8,128)(2,1)} %collective-permute-done.2), channel_id=1, source_target_pairs={{8,0},{9,1},{10,2},{11,3},{12,4},{13,5},{14,6},{15,7},{16,8},{17,9... | collective-permute-start | bytes 4325384 | tf_op jit(solution)/shard_map/ppermute | solution.py:287
  129.1 125.8 %collective-permute-start.8 = (bf16[2,128,2816]{2,1,0:T(8,128)(2,1)}, bf16[2,128,2816]{2,1,0:T(8,128)(2,1)}, u32[]{:S(2)}, u32[]{:S(2)}) collective-permute-start(bf16[2,128,2816]{2,1,0:T(8,128)(2,1)} %broadcast_select_fusion.3.refs_0_), channel_id=1, source_target_pairs={{0,1},{1,0},{2,3},{3,2},{4,5},{5,4},{6,7},{7,6},{8,9},{9,8},{10,11... | collective-permute-start | bytes 4325384 | tf_op jit(solution)/shard_map/ppermute | solution.py:36
  174.8 12.9 %collective-permute-start.5 = (bf16[2,128,2816]{2,1,0:T(8,128)(2,1)}, bf16[2,128,2816]{2,1,0:T(8,128)(2,1)}, u32[]{:S(2)}, u32[]{:S(2)}) collective-permute-start(bf16[2,128,2816]{2,1,0:T(8,128)(2,1)} %collective-permute-done.3), channel_id=1, source_target_pairs={{16,24},{17,25},{18,26},{19,27},{20,28},{21,29},{22,30},{23,31}} | collective-permute-start | bytes 4325384 | tf_op jit(solution)/shard_map/ppermute | solution.py:287
  176.6 34.0 %collective-permute-start.6 = (bf16[2,128,2816]{2,1,0:T(8,128)(2,1)}, bf16[2,128,2816]{2,1,0:T(8,128)(2,1)}, u32[]{:S(2)}, u32[]{:S(2)}) collective-permute-start(bf16[2,128,2816]{2,1,0:T(8,128)(2,1)} %collective-permute-done.4), channel_id=1, source_target_pairs={{8,0},{9,1},{10,2},{11,3},{12,4},{13,5},{14,6},{15,7}} | collective-permute-start | bytes 4325384 | tf_op jit(solution)/shard_map/ppermute | solution.py:287
  180.7 74.1 %collective-permute-start.10 = (bf16[2,128,2816]{2,1,0:T(8,128)(2,1)}, bf16[2,128,2816]{2,1,0:T(8,128)(2,1)}, u32[]{:S(2)}, u32[]{:S(2)}) collective-permute-start(bf16[2,128,2816]{2,1,0:T(8,128)(2,1)} %broadcast_select_fusion.1.refs_4_), channel_id=1, source_target_pairs={{0,1},{1,0},{2,3},{3,2},{4,5},{5,4},{6,7},{7,6},{8,9},{9,8},{10,11... | collective-permute-start | bytes 4325384 | tf_op jit(solution)/shard_map/ppermute | solution.py:36
  210.7 269.8 %reduce-scatter.8.cloned.1.call-start = ((), (), s32[]{:S(2)}) async-start(), calls=%async_computation.7 | async-start | bytes 3604480 | tf_op jit(solution)/shard_map/reduce_scatter | solution.py:320
  213.3 41.6 %collective-permute-start.9 = (bf16[2,128,2816]{2,1,0:T(8,128)(2,1)}, bf16[2,128,2816]{2,1,0:T(8,128)(2,1)}, u32[]{:S(2)}, u32[]{:S(2)}) collective-permute-start(bf16[2,128,2816]{2,1,0:T(8,128)(2,1)} %broadcast_select_fusion.2.refs_2_), channel_id=1, source_target_pairs={{0,1},{1,0},{2,3},{3,2},{4,5},{5,4},{6,7},{7,6},{8,9},{9,8},{10,11... | collective-permute-start | bytes 4325384 | tf_op jit(solution)/shard_map/ppermute | solution.py:36
  219.1 35.8 %collective-permute-start.11 = (bf16[2,128,2816]{2,1,0:T(8,128)(2,1)}, bf16[2,128,2816]{2,1,0:T(8,128)(2,1)}, u32[]{:S(2)}, u32[]{:S(2)}) collective-permute-start(bf16[2,128,2816]{2,1,0:T(8,128)(2,1)} %broadcast_select_fusion.refs_6_), channel_id=1, source_target_pairs={{0,1},{1,0},{2,3},{3,2},{4,5},{5,4},{6,7},{7,6},{8,9},{9,8},{10,11... | collective-permute-start | bytes 4325384 | tf_op jit(solution)/shard_map/ppermute | solution.py:36
  295.2 281.7 %reduce-scatter.4.cloned.1.call-start = ((), (), s32[]{:S(2)}) async-start(), calls=%async_computation.5 | async-start | bytes 3604480 | tf_op jit(solution)/shard_map/reduce_scatter | solution.py:320
  322.7 18.9 %collective-permute-start.17 = (bf16[4,128,2816]{2,1,0:T(8,128)(2,1)}, bf16[4,128,2816]{2,1,0:T(8,128)(2,1)}, u32[]{:S(2)}, u32[]{:S(2)}) collective-permute-start(bf16[4,128,2816]{2,1,0:T(8,128)(2,1)} %dynamic-slice_bitcast_fusion.2), channel_id=1, source_target_pairs={{0,1},{1,0},{2,3},{3,2},{4,5},{5,4},{6,7},{7,6},{8,9},{9,8},{10,11... | collective-permute-start | bytes 8650760 | tf_op jit(solution)/shard_map/ppermute | solution.py:36
  337.3 127.3 %collective-permute-start.19 = (bf16[4,128,2816]{2,1,0:T(8,128)(2,1)}, bf16[4,128,2816]{2,1,0:T(8,128)(2,1)}, u32[]{:S(2)}, u32[]{:S(2)}) collective-permute-start(bf16[4,128,2816]{2,1,0:T(8,128)(2,1)} %dynamic-slice_bitcast_fusion.1), channel_id=1, source_target_pairs={{0,1},{1,0},{2,3},{3,2},{4,5},{5,4},{6,7},{7,6},{8,9},{9,8},{10,11... | collective-permute-start | bytes 8650760 | tf_op jit(solution)/shard_map/ppermute | solution.py:36
  454.8 84.9 %all-to-all-start = ((bf16[8,128,1024]{2,1,0:T(8,128)(2,1)}), bf16[8,128,1024]{2,1,0:T(8,128)(2,1)}, u32[]{:S(2)}, u32[]{:S(2)}) async-start(bf16[8,128,1024]{2,1,0:T(8,128)(2,1)} %bitcast.328), calls=%async_computation | async-start | bytes 4194304 | tf_op jit(solution)/shard_map/all_to_all | solution.py:885
  459.2 126.8 %reduce-scatter.6.cloned.1.call-start = ((), (), s32[]{:S(2)}) async-start(), calls=%async_computation.6 | async-start | bytes 3604480 | tf_op jit(solution)/shard_map/reduce_scatter | solution.py:320
  479.2 19.0 %collective-permute-start.16 = (bf16[8,32,1024]{2,1,0:T(8,128)(2,1)S(1)}, bf16[8,32,1024]{2,1,0:T(8,128)(2,1)}, u32[]{:S(2)}, u32[]{:S(2)}) collective-permute-start(bf16[8,32,1024]{2,1,0:T(8,128)(2,1)S(1)} %dynamic-slice_bitcast_fusion.3), channel_id=1, source_target_pairs={{0,2},{1,3},{2,0},{3,1},{4,6},{5,7},{6,4},{7,5},{8,10},{9,11},{10,... | collective-permute-start | bytes 1572872 | tf_op jit(solution)/shard_map/ppermute | solution.py:36
  480.4 19.2 %collective-permute-start.22 = (bf16[352,1024]{1,0:T(8,128)(2,1)}, bf16[352,1024]{1,0:T(8,128)(2,1)}, u32[]{:S(2)}, u32[]{:S(2)}) collective-permute-start(bf16[352,1024]{1,0:T(8,128)(2,1)} %bitcast.339), channel_id=1, source_target_pairs={{1,4},{3,6},{4,1},{6,3},{9,12},{11,14},{12,9},{14,11},{17,20},{19,... | collective-permute-start | bytes 2162696 | tf_op jit(solution)/shard_map/ppermute | solution.py:54
  576.9 14.8 %collective-permute-start.18 = (bf16[128,2816]{1,0:T(8,128)(2,1)}, bf16[128,2816]{1,0:T(8,128)(2,1)}, u32[]{:S(2)}, u32[]{:S(2)}) collective-permute-start(bf16[128,2816]{1,0:T(8,128)(2,1)} %bitcast.338), channel_id=1, source_target_pairs={{1,4},{3,6},{4,1},{6,3},{9,12},{11,14},{12,9},{14,11},{17,20},{19,... | collective-permute-start | bytes 2162696 | tf_op jit(solution)/shard_map/ppermute | solution.py:54
  586.0 13.3 %collective-permute-start.20 = (bf16[128,2816]{1,0:T(8,128)(2,1)}, bf16[128,2816]{1,0:T(8,128)(2,1)S(1)}, u32[]{:S(2)}, u32[]{:S(2)}) collective-permute-start(bf16[128,2816]{1,0:T(8,128)(2,1)} %bitcast.340), channel_id=1, source_target_pairs={{1,4},{3,6},{4,1},{6,3},{9,12},{11,14},{12,9},{14,11},{17,20},{19,... | collective-permute-start | bytes 2162696 | tf_op jit(solution)/shard_map/ppermute | solution.py:54
  (125 other events, 1378.5 us)
Sparse Core Ops, SparseCore 0:
  15.2 69.1 all-gather.3
  210.8 61.2 all-gather.5
  295.3 53.7 reduce-scatter.7
  351.3 56.0 reduce-scatter.3
  469.0 81.8 reduce-scatter.5

commit v3 on v2

--- a/solution.py
+++ b/solution.py
@@ -727,6 +727,7 @@
     line_round(0)
     seq, gathered = opening(tok, cols)
     seq = line_settle(seq)
+    seq, pair_late = lax.optimization_barrier((seq, pair_own))
     line_round(1)
     seq = seq.reshape(length, D)
     w_qkv = gathered[:, :, : 3 * rows].reshape(EXP_AXIS, cycle, 3, rows, width)
@@ -795,9 +796,9 @@
         preferred_element_type=f32,
     )
     sent_rows = sent_rows.astype(bf16)
-    sent_grads = line_settle(sent_grads.astype(bf16))
-    sent_grads, down_own = lax.optimization_barrier((sent_grads, down_own))
+    sent_grads = sent_grads.astype(bf16)
     got_rows, got_grads = plane_swap((sent_rows.reshape(slots), sent_grads.reshape(slots)), True, 2)
+    got_rows, down_own = lax.optimization_barrier((line_settle(got_rows), down_own))
     for step in range(3, line - 1):
         line_round(step)
     flat_rows = got_rows.reshape(-1, D)
@@ -805,7 +806,7 @@
 
     blocks = []
     for k in range(line):
-        mine = pair_own
+        mine = pair_late
         if k:
             mine = jnp.where(line_place + k < line, left[k], right[line - k])
         blocks += [mine, swap_bit(mine, 0)]
@@ -882,12 +883,20 @@
     dqkv, diag = attend_back(qkv, offset_bias, grad_attended, summed, total)
     partial_normed = jnp.einsum("cte,cde->td", dqkv, w_qkv, preferred_element_type=f32)
     partial_normed = partial_normed.astype(bf16).reshape(cycle, tok_rows, D)
+    dqkv, partial_normed = lax.optimization_barrier((dqkv, partial_normed))
     pieces = lax.all_to_all(partial_normed, "ctx", 0, 0, tiled=True)
     qkv_grad = jnp.einsum("td,cte->cde", normed, dqkv, preferred_element_type=f32)
     qkv_grad = qkv_grad.astype(bf16).reshape(3, cycle, 2, 2, rows, width)
     qkv_grad = qkv_grad.transpose(3, 2, 1, 0, 4, 5)
     qkv_grad = cube_sum(qkv_grad, 0)
     qkv_grad = cube_sum(qkv_grad, 1)
+    expert_results = [
+        adamw_step(master, total[None].astype(f32), first_old, second_old)
+        for master, total, first_old, second_old in zip(
+            masters[6:], (gate_sum, up_sum, down_sum), firsts[6:], seconds[6:]
+        )
+    ]
+    pieces, expert_results = lax.optimization_barrier((pieces, expert_results))
     grad_normed_attn = jnp.sum(pieces.reshape(micro, group, tok_rows, D).astype(f32), axis=1)
     grad_inputs, gain_attn_grad = norm_back(
         inputs, factor_attn, gain_attn, grad_normed_attn.reshape(toks, D)
@@ -929,12 +938,11 @@
         small_sum[edges[1] : edges[2]],
         small_sum[edges[2] : edges[3]],
         small_sum[edges[3] :],
-        *(total[None].astype(f32) for total in (gate_sum, up_sum, down_sum)),
     )
     results = [
         adamw_step(master, gradient, first_old, second_old)
         for master, gradient, first_old, second_old in zip(masters, gradients, firsts, seconds)
-    ]
+    ] + expert_results
     flat = [result[kind] for kind in range(4) for result in results]
     return (output.reshape(tokens.shape), grad_inputs.reshape(tokens.shape), *flat)
 

time: 621 us -> 602 us (0.969)
  the two profiles are of different devices: /device:TPU:5 before, /device:TPU:0 now
where the time goes in v3:
time: 602 us; the launch traced here: 592 us
  Pallas kernels  279 us (46%)
  waiting for transfers between devices  83.2 us (14%)
  other arithmetic  80.3 us (13%)
  matrix products  50.3 us (8%)
  starting transfers between devices  42.3 us (7%)
  local copies, waits for them, and re-layouts  40.7 us (7%)
  between operations  15.9 us (3%)
    pallas_call x6, Pallas kernels, exchange_call(): pl.pallas_call(kernel, in_specs=[vmem] * len(arrays), out_specs=[vmem] *...  202 us
    ppermute x6, waiting for transfers between devices, line_permute(): return lax.ppermute(value, both, pairs)  28 us
    pallas_call x1, Pallas kernels, attend_back(): pl.pallas_call(partial(attend_back_kernel, blocks, heads), grid=(steps,),...  25.4 us
    all_to_all x1, waiting for transfers between devices, layer(): pieces = lax.all_to_all(partial_normed, 'ctx', 0, 0, tiled=True)  24.9 us
    all_gather x1, waiting for transfers between devices, gather_expert(): mine = lax.all_gather(moved, 'ctx', axis=0, axis_index_groups=pair_groups())  20.5 us
    unnamed x182, local copies, waits for them, and re-layouts  20.2 us
    pallas_call x1, Pallas kernels, expert_front(): pl.pallas_call(partial(expert_front_kernel, count), grid=(cols // tile,),...  17.9 us
    mul x8, other arithmetic, adamw_step(): -learn_rate  17.4 us
  transfers between devices with their start and end apart: 29, of which 8 were waited for; matrix products, arithmetic and copies ran while one was open for 24% of the time, Pallas kernels for 43%

profile of v3, /device:TPU:0, one launch (start us, length us, event | category | flops | bytes accessed | tf_op | source)
XLA Modules:
  0.0 591.8 jit_solution(1962205806682164868)
XLA Ops:
  19.9 58.5 %shard_map.590 = (bf16[8,128,1024]{2,1,0:T(8,128)(2,1)S(1)}, bf16[4,8,112,256]{3,2,1,0:T(8,128)(2,1)S(1)}) custom-call(bf16[2,128,1024]{2,1,0:T(8,128)(2,1)S(1)} %bitcast.288, bf16[4,112,256]{2,1,0:T(8,128)(2,1)S(1)} %pad_maximum_fusion.2.col_ref), custom_call_target="tpu_custom_call" | custom-call | bytes 6029312 | tf_op jit(solution)/shard_map/pallas_call | solution.py:79
  82.8 9.5 %collective-permute-start.1 = (bf16[2,128,2816]{2,1,0:T(8,128)(2,1)}, bf16[2,128,2816]{2,1,0:T(8,128)(2,1)}, u32[]{:S(2)}, u32[]{:S(2)}) collective-permute-start(bf16[2,128,2816]{2,1,0:T(8,128)(2,1)} %broadcast_select_fusion.3.refs_0_), channel_id=1, source_target_pairs={{0,8},{1,9},{2,10},{3,11},{4,12},{5,13},{6,14},{7,15},{8,16},{9,17... | collective-permute-start | bytes 4325384 | tf_op jit(solution)/shard_map/ppermute | solution.py:287
  100.3 22.2 %collective-permute-done.1 = bf16[2,128,2816]{2,1,0:T(8,128)(2,1)} collective-permute-done((bf16[2,128,2816]{2,1,0:T(8,128)(2,1)}, bf16[2,128,2816]{2,1,0:T(8,128)(2,1)}, u32[]{:S(2)}, u32[]{:S(2)}) %collective-permute-start.1) | collective-permute-done | bytes 1441824 | tf_op jit(solution)/shard_map/ppermute | solution.py:287
  122.5 5.8 collective-permute-done.2
  137.4 5.2 attend.1
  142.7 34.2 %shard_map.591 = bf16[8,128,256]{2,1,0:T(8,128)(2,1)S(1)} custom-call(bf16[8,128,256]{2,1,0:T(8,128)(2,1)S(1)} %bitcast.302), custom_call_target="tpu_custom_call" | custom-call | bytes 4194304 | tf_op jit(solution)/shard_map/pallas_call | solution.py:79
  189.6 33.6 %shard_map.592 = (bf16[4,2,80,1024]{3,2,1,0:T(8,128)(2,1)S(1)}, bf16[4,2,80,1024]{3,2,1,0:T(8,128)(2,1)S(1)}) custom-call(bf16[4,2,80,1024]{3,2,1,0:T(8,128)(2,1)S(1)} %bitcast.299, bf16[4,2,80,1024]{3,2,1,0:T(8,128)(2,1)S(1)} %bitcast.297), custom_call_target="tpu_custom_call" | custom-call | bytes 20971520 | tf_op jit(solution)/shard_map/pallas_call | solution.py:79
  235.7 17.9 %expert_front.1 = (bf16[640,2816]{1,0:T(8,128)(2,1)}, bf16[640,2816]{1,0:T(8,128)(2,1)}, bf16[640,2816]{1,0:T(8,128)(2,1)}) custom-call(bf16[640,1024]{1,0:T(8,128)(2,1)S(1)} %bitcast.305, bf16[2,128,2816]{2,1,0:T(8,128)(2,1)} %broadcast_select_fusion.3.refs_0_, bf16[2,128,2816]{2,1,0:T(8,128)(2,1)} %collective-permute-done.8.refs_1_, ...), custom_call_target="tpu_custom_call" | custom-call | flops 7381975040 | bytes 11534336 | tf_op jit(solution)/shard_map/expert_front/pallas_call | solution.py:367
  253.6 7.0 %convolution_convert_fusion = bf16[2816,1024]{1,0:T(8,128)(2,1)S(1)} fusion(bf16[640,2816]{1,0:T(8,128)(2,1)} %get-tuple-element.101, bf16[640,1024]{1,0:T(8,128)(2,1)S(1)} %bitcast.294), kind=kOutput, calls=%fused_computation.7 | convolution fusion | flops 3693871104 | bytes 10682368 | tf_op jit(solution)/shard_map/dot_general | solution.py:835
  264.6 20.5 %all-gather.6.cloned.1.call-done = bf16[1408,1024]{1,0:T(8,128)(2,1)} async-done(((bf16[352,1024]{1,0:T(8,128)(2,1)}), bf16[1408,1024]{1,0:T(8,128)(2,1)}) %all-gather.6.cloned.1.call-update) | async-done | bytes 2883600 | tf_op jit(solution)/shard_map/all_gather | solution.py:303
  285.2 5.7 fusion
  297.1 12.6 %expert_middle.1 = (bf16[640,2816]{1,0:T(8,128)(2,1)S(1)}, bf16[640,2816]{1,0:T(8,128)(2,1)}) custom-call(bf16[640,1024]{1,0:T(8,128)(2,1)S(1)} %bitcast.295, bf16[2816,1024]{1,0:T(8,128)(2,1)} %bitcast.307, bf16[640,2816]{1,0:T(8,128)(2,1)} %get-tuple-element.104.value_ref, bf16[640,2816]{1,0:T(8,128)(2,1)} %get-tuple-element.105.slope_ref), custom_call_target="tpu_custom_call" | custom-call | flops 3690987520 | bytes 5767168 | tf_op jit(solution)/shard_map/expert_middle/pallas_call | solution.py:392
  309.7 8.3 %convolution_convert_fusion.1 = bf16[1024,2816]{1,0:T(8,128)(2,1)S(1)} fusion(bf16[640,1024]{1,0:T(8,128)(2,1)S(1)} %bitcast.306, bf16[640,2816]{1,0:T(8,128)(2,1)} %get-tuple-element.107.up_ref), kind=kOutput, calls=%fused_computation.8 | convolution fusion | flops 3693871104 | bytes 10682368 | tf_op jit(solution)/shard_map/dot_general | solution.py:838
  335.3 6.6 %convolution_convert_fusion.2 = bf16[1024,2816]{1,0:T(8,128)(2,1)S(1)} fusion(bf16[640,1024]{1,0:T(8,128)(2,1)} %bitcast.304, bf16[640,2816]{1,0:T(8,128)(2,1)S(1)} %copy-done.9), kind=kOutput, calls=%fused_computation.9 | convolution fusion | flops 3693871104 | bytes 10682368 | tf_op jit(solution)/shard_map/dot_general | solution.py:840
  346.6 15.9 %expert_rear.1 = bf16[640,1024]{1,0:T(8,128)(2,1)S(1)} custom-call(bf16[640,2816]{1,0:T(8,128)(2,1)} %copy-done.8, bf16[640,2816]{1,0:T(8,128)(2,1)} %get-tuple-element.107.up_ref, bf16[2,128,2816]{2,1,0:T(8,128)(2,1)} %broadcast_select_fusion.3.refs_0_, bf16[2,128,2816]{2,1,0:T(8,128)(2,1)} %collective-permute-done.8.refs_1_, ...), custom_call_target="tpu_custom_call" | custom-call | flops 7381975040 | bytes 11534336 | tf_op jit(solution)/shard_map/expert_rear/pallas_call | solution.py:439
  362.6 5.9 convolution_convert_fusion.6
  368.5 29.4 %shard_map.593 = (bf16[4,2,80,1024]{3,2,1,0:T(8,128)(2,1)S(1)}, bf16[4,2,80,1024]{3,2,1,0:T(8,128)(2,1)S(1)}) custom-call(bf16[4,2,80,1024]{3,2,1,0:T(8,128)(2,1)S(1)} %bitcast.298, bf16[4,2,80,1024]{3,2,1,0:T(8,128)(2,1)S(1)} %bitcast.296), custom_call_target="tpu_custom_call" | custom-call | bytes 20971520 | tf_op jit(solution)/shard_map/pallas_call | solution.py:79
  410.6 22.4 %shard_map.594 = bf16[8,128,256]{2,1,0:T(8,128)(2,1)S(1)} custom-call(bf16[8,128,256]{2,1,0:T(8,128)(2,1)S(1)} %bitcast.293), custom_call_target="tpu_custom_call" | custom-call | bytes 4194304 | tf_op jit(solution)/shard_map/pallas_call | solution.py:79
  433.8 25.4 %attend_back.1 = (bf16[3,1024,256]{2,1,0:T(8,128)(2,1)}, f32[2,8,512]{2,1,0:T(8,128)}) custom-call(bf16[3,1024,256]{2,1,0:T(8,128)(2,1)} %copy-done.13, f32[2,2,2048]{2,1,0:T(2,128)} %copy-done.7, bf16[1024,256]{1,0:T(8,128)(2,1)} %bitcast.301, f32[1024,256]{1,0:T(8,128)} %copy-done.14, f32[1024,256]{1,0:T(8,128)} %copy-done.15), custom_call_target="tpu_custom_call" | custom-call | flops 2684354560 | bytes 7864320 | tf_op jit(solution)/shard_map/attend_back/pallas_call | solution.py:635
  489.0 10.4 %all-to-all-start = ((bf16[8,128,1024]{2,1,0:T(8,128)(2,1)}), bf16[8,128,1024]{2,1,0:T(8,128)(2,1)}, u32[]{:S(2)}, u32[]{:S(2)}) async-start(bf16[8,128,1024]{2,1,0:T(8,128)(2,1)} %bitcast.326), calls=%async_computation | async-start | bytes 4194304 | tf_op jit(solution)/shard_map/all_to_all | solution.py:887
  505.4 5.4 add_multiply_fusion
  513.1 5.3 add_multiply_fusion.1
  524.5 24.9 %all-to-all-done = bf16[8,128,1024]{2,1,0:T(8,128)(2,1)} async-done(((bf16[8,128,1024]{2,1,0:T(8,128)(2,1)}), bf16[8,128,1024]{2,1,0:T(8,128)(2,1)}, u32[]{:S(2)}, u32[]{:S(2)}) %all-to-all-start) | async-done | bytes 2097184 | tf_op jit(solution)/shard_map/all_to_all | solution.py:887
  553.2 24.2 %shard_map.595 = (bf16[8,3,32,256]{3,2,1,0:T(8,128)(2,1)S(1)}, bf16[8,32,1024]{2,1,0:T(8,128)(2,1)S(1)}, f32[8,4,1,256]{3,2,1,0:T(1,128)}, f32[4,8,4,1,256]{4,3,2,1,0:T(1,128)S(1)}) custom-call(bf16[8,3,32,256]{3,2,1,0:T(8,128)(2,1)S(1)} %fusion.46.col_ref, bf16[8,32,1024]{2,1,0:T(8,128)(2,1)S(1)} %fusion.38.out_in, f32[8,4,1,256]{3,2,1,0:T(1,128)S(1)} %reshape.461.small_ref), custom_call_target="tpu_custom_call" | custom-call | bytes 7602176 | tf_op jit(solution)/shard_map/pallas_call | solution.py:79
  (383 shorter events, 159.3 us)
Async XLA Ops:
  7.2 170.3 %all-gather.4.cloned.1.call-start = ((), (), s32[]{:S(2)}) async-start(), calls=%async_computation.4 | async-start | bytes 2162688 | tf_op jit(solution)/shard_map/all_gather | solution.py:714
  10.6 69.4 %collective-permute-start = (bf16[2,128,2816]{2,1,0:T(8,128)(2,1)}, bf16[2,128,2816]{2,1,0:T(8,128)(2,1)}, u32[]{:S(2)}, u32[]{:S(2)}) collective-permute-start(bf16[2,128,2816]{2,1,0:T(8,128)(2,1)} %pad_maximum_fusion.1), channel_id=1, source_target_pairs={{1,4},{3,6},{4,1},{6,3},{9,12},{11,14},{12,9},{14,11},{17,20},{19,... | collective-permute-start | bytes 4325384 | tf_op jit(solution)/shard_map/ppermute | solution.py:54
  13.2 271.9 %all-gather.6.cloned.1.call-start = ((), (), s32[]{:S(2)}) async-start(), calls=%async_computation.8 | async-start | bytes 3604480 | tf_op jit(solution)/shard_map/all_gather | solution.py:303
  14.2 117.1 %collective-permute-start.7 = (bf16[352,1024]{1,0:T(8,128)(2,1)}, bf16[352,1024]{1,0:T(8,128)(2,1)}, u32[]{:S(2)}, u32[]{:S(2)}) collective-permute-start(bf16[352,1024]{1,0:T(8,128)(2,1)} %convert_bitcast_fusion.3), channel_id=1, source_target_pairs={{1,4},{3,6},{4,1},{6,3},{9,12},{11,14},{12,9},{14,11},{17,20},{19,... | collective-permute-start | bytes 2162696 | tf_op jit(solution)/shard_map/ppermute | solution.py:54
  82.8 39.7 %collective-permute-start.1 = (bf16[2,128,2816]{2,1,0:T(8,128)(2,1)}, bf16[2,128,2816]{2,1,0:T(8,128)(2,1)}, u32[]{:S(2)}, u32[]{:S(2)}) collective-permute-start(bf16[2,128,2816]{2,1,0:T(8,128)(2,1)} %broadcast_select_fusion.3.refs_0_), channel_id=1, source_target_pairs={{0,8},{1,9},{2,10},{3,11},{4,12},{5,13},{6,14},{7,15},{8,16},{9,17... | collective-permute-start | bytes 4325384 | tf_op jit(solution)/shard_map/ppermute | solution.py:287
  92.3 36.1 %collective-permute-start.2 = (bf16[2,128,2816]{2,1,0:T(8,128)(2,1)}, bf16[2,128,2816]{2,1,0:T(8,128)(2,1)}, u32[]{:S(2)}, u32[]{:S(2)}) collective-permute-start(bf16[2,128,2816]{2,1,0:T(8,128)(2,1)} %broadcast_select_fusion.3.refs_0_), channel_id=1, source_target_pairs={{8,0},{9,1},{10,2},{11,3},{12,4},{13,5},{14,6},{15,7},{16,8},{17,9... | collective-permute-start | bytes 4325384 | tf_op jit(solution)/shard_map/ppermute | solution.py:287
  128.3 48.6 %collective-permute-start.3 = (bf16[2,128,2816]{2,1,0:T(8,128)(2,1)}, bf16[2,128,2816]{2,1,0:T(8,128)(2,1)}, u32[]{:S(2)}, u32[]{:S(2)}) collective-permute-start(bf16[2,128,2816]{2,1,0:T(8,128)(2,1)} %collective-permute-done.1), channel_id=1, source_target_pairs={{8,16},{9,17},{10,18},{11,19},{12,20},{13,21},{14,22},{15,23},{16,... | collective-permute-start | bytes 4325384 | tf_op jit(solution)/shard_map/ppermute | solution.py:287
  130.1 46.8 %collective-permute-start.4 = (bf16[2,128,2816]{2,1,0:T(8,128)(2,1)}, bf16[2,128,2816]{2,1,0:T(8,128)(2,1)}, u32[]{:S(2)}, u32[]{:S(2)}) collective-permute-start(bf16[2,128,2816]{2,1,0:T(8,128)(2,1)} %collective-permute-done.2), channel_id=1, source_target_pairs={{8,0},{9,1},{10,2},{11,3},{12,4},{13,5},{14,6},{15,7},{16,8},{17,9... | collective-permute-start | bytes 4325384 | tf_op jit(solution)/shard_map/ppermute | solution.py:287
  176.8 54.3 %collective-permute-start.8 = (bf16[2,128,2816]{2,1,0:T(8,128)(2,1)}, bf16[2,128,2816]{2,1,0:T(8,128)(2,1)}, u32[]{:S(2)}, u32[]{:S(2)}) collective-permute-start(bf16[2,128,2816]{2,1,0:T(8,128)(2,1)} %broadcast_select_fusion.3.refs_0_), channel_id=1, source_target_pairs={{0,1},{1,0},{2,3},{3,2},{4,5},{5,4},{6,7},{7,6},{8,9},{9,8},{10,11... | collective-permute-start | bytes 4325384 | tf_op jit(solution)/shard_map/ppermute | solution.py:36
  180.1 45.2 %collective-permute-start.5 = (bf16[2,128,2816]{2,1,0:T(8,128)(2,1)}, bf16[2,128,2816]{2,1,0:T(8,128)(2,1)}, u32[]{:S(2)}, u32[]{:S(2)}) collective-permute-start(bf16[2,128,2816]{2,1,0:T(8,128)(2,1)} %collective-permute-done.3), channel_id=1, source_target_pairs={{16,24},{17,25},{18,26},{19,27},{20,28},{21,29},{22,30},{23,31}} | collective-permute-start | bytes 4325384 | tf_op jit(solution)/shard_map/ppermute | solution.py:287
  181.9 43.4 %collective-permute-start.6 = (bf16[2,128,2816]{2,1,0:T(8,128)(2,1)}, bf16[2,128,2816]{2,1,0:T(8,128)(2,1)}, u32[]{:S(2)}, u32[]{:S(2)}) collective-permute-start(bf16[2,128,2816]{2,1,0:T(8,128)(2,1)} %collective-permute-done.4), channel_id=1, source_target_pairs={{8,0},{9,1},{10,2},{11,3},{12,4},{13,5},{14,6},{15,7}} | collective-permute-start | bytes 4325384 | tf_op jit(solution)/shard_map/ppermute | solution.py:287
  186.0 45.1 %collective-permute-start.10 = (bf16[2,128,2816]{2,1,0:T(8,128)(2,1)}, bf16[2,128,2816]{2,1,0:T(8,128)(2,1)}, u32[]{:S(2)}, u32[]{:S(2)}) collective-permute-start(bf16[2,128,2816]{2,1,0:T(8,128)(2,1)} %broadcast_select_fusion.1.refs_4_), channel_id=1, source_target_pairs={{0,1},{1,0},{2,3},{3,2},{4,5},{5,4},{6,7},{7,6},{8,9},{9,8},{10,11... | collective-permute-start | bytes 4325384 | tf_op jit(solution)/shard_map/ppermute | solution.py:36
  225.3 259.9 %reduce-scatter.8.cloned.1.call-start = ((), (), s32[]{:S(2)}) async-start(), calls=%async_computation.7 | async-start | bytes 3604480 | tf_op jit(solution)/shard_map/reduce_scatter | solution.py:320
  264.2 21.0 %collective-permute-start.17 = (bf16[4,352,1024]{2,1,0:T(8,128)(2,1)}, bf16[4,352,1024]{2,1,0:T(8,128)(2,1)}, u32[]{:S(2)}, u32[]{:S(2)}) collective-permute-start(bf16[4,352,1024]{2,1,0:T(8,128)(2,1)} %dynamic-slice_bitcast_fusion), channel_id=1, source_target_pairs={{0,1},{1,0},{2,3},{3,2},{4,5},{5,4},{6,7},{7,6},{8,9},{9,8},{10,11... | collective-permute-start | bytes 8650760 | tf_op jit(solution)/shard_map/ppermute | solution.py:36
  290.9 213.0 %reduce-scatter.6.cloned.1.call-start = ((), (), s32[]{:S(2)}) async-start(), calls=%async_computation.6 | async-start | bytes 3604480 | tf_op jit(solution)/shard_map/reduce_scatter | solution.py:320
  332.1 180.0 %reduce-scatter.4.cloned.1.call-start = ((), (), s32[]{:S(2)}) async-start(), calls=%async_computation.5 | async-start | bytes 3604480 | tf_op jit(solution)/shard_map/reduce_scatter | solution.py:320
  346.2 57.0 %collective-permute-start.13 = (bf16[4,128,2816]{2,1,0:T(8,128)(2,1)}, bf16[4,128,2816]{2,1,0:T(8,128)(2,1)}, u32[]{:S(2)}, u32[]{:S(2)}) collective-permute-start(bf16[4,128,2816]{2,1,0:T(8,128)(2,1)} %dynamic-slice_bitcast_fusion.2), channel_id=1, source_target_pairs={{0,1},{1,0},{2,3},{3,2},{4,5},{5,4},{6,7},{7,6},{8,9},{9,8},{10,11... | collective-permute-start | bytes 8650760 | tf_op jit(solution)/shard_map/ppermute | solution.py:36
  474.9 6.7 %collective-permute-start.21 = (bf16[2,8,32,1024]{3,2,1,0:T(8,128)(2,1)}, bf16[2,8,32,1024]{3,2,1,0:T(8,128)(2,1)}, u32[]{:S(2)}, u32[]{:S(2)}) collective-permute-start(bf16[2,8,32,1024]{3,2,1,0:T(8,128)(2,1)} %bitcast.280), channel_id=1, source_target_pairs={{0,1},{1,0},{2,3},{3,2},{4,5},{5,4},{6,7},{7,6},{8,9},{9,8},{10,11... | collective-permute-start | bytes 3145736 | tf_op jit(solution)/shard_map/ppermute | solution.py:36
  479.7 20.4 %collective-permute-start.20 = (bf16[8,3,32,256]{3,2,1,0:T(8,128)(2,1)}, bf16[8,3,32,256]{3,2,1,0:T(8,128)(2,1)}, u32[]{:S(2)}, u32[]{:S(2)}) collective-permute-start(bf16[8,3,32,256]{3,2,1,0:T(8,128)(2,1)} %dynamic-slice_bitcast_fusion.4), channel_id=1, source_target_pairs={{0,2},{1,3},{2,0},{3,1},{4,6},{5,7},{6,4},{7,5},{8,10},{9,11},{10,... | collective-permute-start | bytes 1179656 | tf_op jit(solution)/shard_map/ppermute | solution.py:36
  485.1 17.5 %collective-permute-start.22 = (bf16[8,32,1024]{2,1,0:T(8,128)(2,1)}, bf16[8,32,1024]{2,1,0:T(8,128)(2,1)}, u32[]{:S(2)}, u32[]{:S(2)}) collective-permute-start(bf16[8,32,1024]{2,1,0:T(8,128)(2,1)} %dynamic-slice_bitcast_fusion.3), channel_id=1, source_target_pairs={{0,2},{1,3},{2,0},{3,1},{4,6},{5,7},{6,4},{7,5},{8,10},{9,11},{10,... | collective-permute-start | bytes 1572872 | tf_op jit(solution)/shard_map/ppermute | solution.py:36
  485.2 20.2 %collective-permute-start.18 = (bf16[352,1024]{1,0:T(8,128)(2,1)}, bf16[352,1024]{1,0:T(8,128)(2,1)}, u32[]{:S(2)}, u32[]{:S(2)}) collective-permute-start(bf16[352,1024]{1,0:T(8,128)(2,1)} %bitcast.336), channel_id=1, source_target_pairs={{1,4},{3,6},{4,1},{6,3},{9,12},{11,14},{12,9},{14,11},{17,20},{19,... | collective-permute-start | bytes 2162696 | tf_op jit(solution)/shard_map/ppermute | solution.py:54
  489.0 60.5 %all-to-all-start = ((bf16[8,128,1024]{2,1,0:T(8,128)(2,1)}), bf16[8,128,1024]{2,1,0:T(8,128)(2,1)}, u32[]{:S(2)}, u32[]{:S(2)}) async-start(bf16[8,128,1024]{2,1,0:T(8,128)(2,1)} %bitcast.326), calls=%async_computation | async-start | bytes 4194304 | tf_op jit(solution)/shard_map/all_to_all | solution.py:887
  503.9 9.2 %collective-permute-start.16 = (bf16[128,2816]{1,0:T(8,128)(2,1)}, bf16[128,2816]{1,0:T(8,128)(2,1)}, u32[]{:S(2)}, u32[]{:S(2)}) collective-permute-start(bf16[128,2816]{1,0:T(8,128)(2,1)} %bitcast.337), channel_id=1, source_target_pairs={{1,4},{3,6},{4,1},{6,3},{9,12},{11,14},{12,9},{14,11},{17,20},{19,... | collective-permute-start | bytes 2162696 | tf_op jit(solution)/shard_map/ppermute | solution.py:54
  512.1 7.5 %collective-permute-start.14 = (bf16[128,2816]{1,0:T(8,128)(2,1)}, bf16[128,2816]{1,0:T(8,128)(2,1)S(1)}, u32[]{:S(2)}, u32[]{:S(2)}) collective-permute-start(bf16[128,2816]{1,0:T(8,128)(2,1)} %bitcast.338), channel_id=1, source_target_pairs={{1,4},{3,6},{4,1},{6,3},{9,12},{11,14},{12,9},{14,11},{17,20},{19,... | collective-permute-start | bytes 2162696 | tf_op jit(solution)/shard_map/ppermute | solution.py:54
  (92 other events, 492.6 us)
Sparse Core Ops, SparseCore 0:
  13.3 73.1 all-gather.3
  225.4 59.6 all-gather.5
  291.0 55.1 reduce-scatter.7
  348.4 56.0 reduce-scatter.5
  407.5 65.3 reduce-scatter.3
